TPU v7x, 256 devices: a whole 4x4x8 slice. The times are simulated.
256 devices in a mesh: lat: 32 (over y_hi, z, core), lon: 8 (over y_lo, x).
Axes of the slice: x: 4, y: 4 (y_hi: 2, y_lo: 2; y = y_hi * 2 + y_lo), z: 8, core: 2. Of those that a mesh axis runs over, the one named last changes fastest.
Arguments:
- field: bfloat16 [384, 768, 512], P('lat', 'lon'), may hold values from -6 to 6
- quad_weight: float32 [384], P('lat'), may hold values from 0.5 to 1.5
- legendre: bfloat16 [384, 384, 384], P('lat'), as said below
- filter_real: float32 [384, 512], replicated, may hold values from -4 to 4
- filter_imag: float32 [384, 512], replicated, may hold values from -4 to 4
- neighbour: int32 [384, 12], P('lat'), may hold values from 0 to 24
- basis: int32 [384, 12], P('lat'), may hold values from 0 to 7
- disco_quad: float32 [384, 12], P('lat'), may hold values from 0.5 to 1.5
- disco_weight: float32 [8, 512], replicated, may hold values from -2 to 2
- norm_gain: float32 [512], replicated, may hold values from 0.5 to 1.5
- w_in: bfloat16 [512, 1024], replicated, may hold values from -0.25 to 0.25
- b_in: float32 [1024], replicated, may hold values from -3 to 3
- w_out: bfloat16 [1024, 512], replicated, may hold values from -0.1875 to 0.1875
- b_out: float32 [512], replicated, may hold values from -3 to 3
Outputs:
- block_out: bfloat16 [384, 768, 512], P('lat', 'lon')
- spatial: bfloat16 [384, 768, 512], P('lat', 'lon')
Inputs may be any that keep to these rules, and one draw needn't show every extreme that they name: legendre[m, l, t] = 0 for l < m.
All inputs are finite; a program needn't handle non-finite values.
Results may differ from a plain program's by a relative error of at most 0.018.
Values may be sent and summed in bfloat16 or wider, within the bound.
A program may use at most 64 MiB of HBM per device.

v0:
```python
import math

import jax
import jax.numpy as jnp
from jax import lax
from jax.sharding import PartitionSpec as P

HALO = 2
KB = 8
NWIN = 25


exact_mode = lax.Precision.HIGHEST


def padded_2(block, sides, width):
    for axis, dim in sides:
        count = lax.axis_size(axis)
        forward = [(i, i + 1) for i in range(count - 1)]
        backward = [(target, source) for source, target in forward]
        low = lax.ppermute(
            lax.slice_in_dim(block, block.shape[dim] - width, None, axis=dim), axis, forward
        )
        high = lax.ppermute(lax.slice_in_dim(block, 0, width, axis=dim), axis, backward)
        block = jnp.concatenate([low, block, high], axis=dim)
    return block


def split_table(table):
    upper = table.astype(jnp.bfloat16)
    lower = (table - upper.astype(jnp.float32)).astype(jnp.bfloat16)
    return (upper, lower)


def fourier_tables(nlon, mmax):
    points = jnp.arange(nlon, dtype=jnp.int32)
    waves = jnp.arange(mmax, dtype=jnp.int32)
    phase = waves[:, None] * points[None, :] % nlon
    angle = phase.astype(jnp.float32) * (2.0 * math.pi / nlon)
    cosine = jnp.cos(angle) / math.sqrt(nlon)
    sine = jnp.sin(angle) / math.sqrt(nlon)
    forward_table = jnp.stack([cosine, -sine], axis=0)
    factor = jnp.where(waves == 0, 1.0, 2.0).astype(jnp.float32)[:, None]
    inverse_table = jnp.stack([factor * cosine, -factor * sine], axis=0)
    return (forward_table, inverse_table)


def window_kernel(neighbour, basis, disco_quad, weight_cols):
    places = (neighbour[:, :, None] == jnp.arange(NWIN, dtype=jnp.int32)[None, None, :]).astype(
        jnp.float32
    )
    places = places * disco_quad[:, :, None]
    kinds = (basis[:, :, None] == jnp.arange(KB, dtype=jnp.int32)[None, None, :]).astype(
        jnp.float32
    )
    mixing = jnp.einsum("isn,isb->inb", places, kinds, precision=exact_mode)
    return jnp.einsum("inb,bc->inc", mixing, weight_cols, precision=exact_mode)


def convolve(padded, kernel, lat_rows, lon_cols):
    span = 2 * HALO + 1
    total = jnp.zeros((lat_rows, lon_cols, kernel.shape[2]), jnp.float32)
    for offset in range(NWIN):
        row_shift = offset // span
        col_shift = offset % span
        window = padded[row_shift : row_shift + lat_rows, col_shift : col_shift + lon_cols, :]
        total = total + kernel[:, offset, None, :] * window
    return total


def channel_mlp(spatial, field, norm_gain, w_in, b_in, w_out, b_out):
    channels = spatial.shape[-1]
    tokens = spatial.reshape(-1, channels).astype(jnp.float32)
    center = jnp.mean(tokens, axis=1, keepdims=True)
    spread = jnp.mean((tokens - center) ** 2, axis=1, keepdims=True)
    normed = ((tokens - center) * lax.rsqrt(spread + 1e-05) * norm_gain).astype(jnp.bfloat16)
    hidden = jnp.dot(normed, w_in, preferred_element_type=jnp.float32) + b_in
    hidden = jax.nn.gelu(hidden).astype(jnp.bfloat16)
    result = jnp.dot(hidden, w_out, preferred_element_type=jnp.float32)
    result = result + b_out + field.reshape(-1, channels).astype(jnp.float32)
    return result.astype(jnp.bfloat16).reshape(field.shape)


def shards(
    field,
    quad_weight,
    legendre,
    filter_real,
    filter_imag,
    neighbour,
    basis,
    disco_quad,
    disco_weight,
    norm_gain,
    w_in,
    b_in,
    w_out,
    b_out,
):
    lat_rows, lon_cols, channels = field.shape
    lon_count = lax.axis_size("lon")
    lat_count = lax.axis_size("lat")
    nlon = lon_cols * lon_count
    wave_block = legendre.shape[0]
    mmax = wave_block * lat_count
    cblock = channels // lon_count
    forward_table, inverse_table = fourier_tables(nlon, mmax)
    forward_upper, forward_lower = split_table(forward_table)
    inverse_upper, inverse_lower = split_table(inverse_table)
    columns = lax.all_to_all(field, "lon", split_axis=2, concat_axis=1, tiled=True)
    frequency = jnp.einsum(
        "tkc,rmk->rmtc", columns, forward_upper, preferred_element_type=jnp.float32
    )
    frequency = frequency + jnp.einsum(
        "tkc,rmk->rmtc", columns, forward_lower, preferred_element_type=jnp.float32
    )
    weighted = (frequency * quad_weight[None, None, :, None]).astype(jnp.bfloat16)
    weighted = jnp.transpose(weighted, (1, 2, 0, 3))
    coeffs = jnp.einsum(
        "mlt,mtrc->mlrc",
        legendre,
        lax.all_to_all(weighted, "lat", split_axis=0, concat_axis=1, tiled=True),
        preferred_element_type=jnp.float32,
    )
    chan_start = lax.axis_index("lon") * cblock
    gain_real = lax.dynamic_slice_in_dim(filter_real, chan_start, cblock, 1)[None, :, :]
    gain_imag = lax.dynamic_slice_in_dim(filter_imag, chan_start, cblock, 1)[None, :, :]
    real_part = coeffs[:, :, 0]
    imag_part = coeffs[:, :, 1]
    filtered = jnp.stack(
        [
            gain_real * real_part - gain_imag * imag_part,
            gain_real * imag_part + gain_imag * real_part,
        ],
        axis=2,
    ).astype(jnp.bfloat16)
    synthesis = jnp.einsum(
        "mlt,mlrc->mtrc", legendre, filtered, preferred_element_type=jnp.float32
    ).astype(jnp.bfloat16)
    lat_block = lax.all_to_all(synthesis, "lat", split_axis=1, concat_axis=0, tiled=True)
    wave = jnp.einsum("mtrc,rmk->tkc", lat_block, inverse_upper, preferred_element_type=jnp.float32)
    wave = wave + jnp.einsum(
        "mtrc,rmk->tkc", lat_block, inverse_lower, preferred_element_type=jnp.float32
    )
    wave = wave.astype(jnp.bfloat16)
    weight_cols = lax.dynamic_slice_in_dim(disco_weight, chan_start, cblock, 1)
    kernel = window_kernel(neighbour, basis, disco_quad, weight_cols)
    cycle = jnp.concatenate([wave[:, nlon - HALO :], wave, wave[:, :HALO]], axis=1)
    padded = padded_2(cycle, (("lat", 0),), HALO)
    conv = convolve(padded, kernel, lat_rows, nlon)
    spatial_part = (wave.astype(jnp.float32) + conv).astype(jnp.bfloat16)
    spatial = lax.all_to_all(spatial_part, "lon", split_axis=1, concat_axis=2, tiled=True)
    block_out = channel_mlp(spatial, field, norm_gain, w_in, b_in, w_out, b_out)
    return (block_out, spatial)


def solution(mesh):
    placed = (
        P("lat", "lon", None),
        P("lat"),
        P("lat", None, None),
        P(),
        P(),
        P("lat", None),
        P("lat", None),
        P("lat", None),
        P(),
        P(),
        P(),
        P(),
        P(),
        P(),
    )
    return jax.shard_map(
        shards,
        mesh=mesh,
        in_specs=placed,
        out_specs=(P("lat", "lon", None), P("lat", "lon", None)),
        check_vma=False,
    )
```

profile of v0, /device:TPU:1, one launch (start us, length us, event | category | flops | bytes accessed | tf_op | source)
XLA Modules:
  0.0 265.8 jit_solution(6598086077392066688)
XLA Ops:
  0.6 4.5 %copy.55 = bf16[12,96,512]{1,0,2:T(8,128)(2,1)} copy(bf16[12,96,512]{2,1,0:T(8,128)(2,1)} %param.14) | data formatting | bytes 2359296 | tf_op args[0]
  5.1 5.9 %all-to-all-start = ((bf16[12,96,512]{1,0,2:T(8,128)(2,1)}), bf16[12,96,512]{1,0,2:T(8,128)(2,1)}, u32[]{:S(2)}, u32[]{:S(2)}) async-start(bf16[12,96,512]{1,0,2:T(8,128)(2,1)} %copy.55), calls=%async_computation | async-start | bytes 4194304 | tf_op jit(solution)/shard_map/all_to_all | solution.py:110
  11.0 6.4 %multiply_negate_fusion = (f32[1,384,768]{2,1,0:T(8,128)}, f32[1,384,768]{2,1,0:T(8,128)}) fusion(), kind=kLoop, calls=%fused_computation.79 | loop fusion | flops 3538944 | bytes 2359296 | tf_op jit(solution)/shard_map/neg | solution.py:42
  17.3 20.8 %all-to-all-done = bf16[12,96,512]{1,0,2:T(8,128)(2,1)} async-done(((bf16[12,96,512]{1,0,2:T(8,128)(2,1)}), bf16[12,96,512]{1,0,2:T(8,128)(2,1)}, u32[]{:S(2)}, u32[]{:S(2)}) %all-to-all-start) | async-done | bytes 1179680 | tf_op jit(solution)/shard_map/all_to_all | solution.py:110
  38.2 3.8 %copy.57 = bf16[12,8,96,64]{2,1,3,0:T(8,128)(2,1)} copy(bf16[12,8,96,64]{2,0,3,1:T(8,128)(2,1)} %bitcast.4) | data formatting | bytes 2359296 | tf_op jit(solution)/shard_map/all_to_all | solution.py:110
  42.0 3.8 %reshape.182 = bf16[12,768,64,1]{1,2,0,3:T(8,128)(2,1)} reshape(bf16[12,8,96,64]{2,1,3,0:T(8,128)(2,1)} %copy.57) | data formatting | bytes 2359296 | tf_op jit(solution)/shard_map/all_to_all | solution.py:110
  45.8 3.2 %fusion.48 = f32[2,384,12,64]{1,3,2,0:T(8,128)S(1)} fusion(bf16[12,768,64,1]{1,2,0,3:T(8,128)(2,1)} %reshape.182, f32[1,384,768]{2,1,0:T(8,128)} %get-tuple-element.41, f32[1,384,768]{2,1,0:T(8,128)} %get-tuple-element.42), kind=kOutput, calls=%fused_computation.61 | convolution fusion | flops 908328960 | bytes 5898240 | tf_op jit(solution)/shard_map/tkc,rmk->rmtc/dot_general | solution.py:111
  49.1 2.2 fusion.41
  51.2 6.7 %copy.58 = bf16[384,12,2,64]{3,2,1,0:T(2,128)(2,1)} copy(bf16[384,12,2,64]{0,3,1,2:T(8,128)(2,1)} %fusion.41) | data formatting | bytes 2359296 | tf_op jit(solution)/shard_map/convert_element_type | solution.py:117
  57.9 6.3 %reshape.191 = bf16[32,2,9216]{2,1,0:T(2,128)(2,1)} reshape(bf16[384,12,2,64]{3,2,1,0:T(2,128)(2,1)} %copy.58) | data formatting | bytes 2359296
  64.2 11.9 %all-to-all-start.1 = ((bf16[32,2,9216]{2,1,0:T(2,128)(2,1)}), bf16[32,2,9216]{2,1,0:T(2,128)(2,1)}, u32[]{:S(2)}, u32[]{:S(2)}) async-start(bf16[32,2,9216]{2,1,0:T(2,128)(2,1)} %reshape.191), calls=%async_computation.1 | async-start | bytes 2359296 | tf_op jit(solution)/shard_map/all_to_all | solution.py:122
  76.2 2.0 constant_dynamic-slice_fusion
  78.1 1.7 copy.61
  79.8 1.7 copy.54
  81.5 1.0 fusion.74
  82.5 1.2 fusion.80
  83.7 0.7 copy-done.8
  84.4 0.7 fusion.96
  85.1 0.6 copy.132
  85.7 0.6 select_multiply_fusion
  86.3 0.6 fusion.83
  86.8 0.6 copy_bitcast_fusion.2
  87.4 0.6 copy_bitcast_fusion.4
  88.1 18.7 %all-to-all-done.1 = bf16[32,2,9216]{2,1,0:T(2,128)(2,1)} async-done(((bf16[32,2,9216]{2,1,0:T(2,128)(2,1)}), bf16[32,2,9216]{2,1,0:T(2,128)(2,1)}, u32[]{:S(2)}, u32[]{:S(2)}) %all-to-all-start.1) | async-done | bytes 1179680 | tf_op jit(solution)/shard_map/all_to_all | solution.py:122
  106.7 6.3 %reshape.192 = bf16[384,12,2,64]{3,2,1,0:T(2,128)(2,1)} reshape(bf16[32,2,9216]{2,1,0:T(2,128)(2,1)} %all-to-all-done.1) | data formatting | bytes 2359296
  113.0 3.7 %copy.59 = bf16[12,32,12,2,64]{4,3,2,1,0:T(2,128)(2,1)S(1)} copy(bf16[12,32,12,2,64]{4,3,2,0,1:T(2,128)(2,1)} %bitcast.148) | data formatting | bytes 2359296 | tf_op jit(solution)/shard_map/all_to_all | solution.py:122
  116.7 1.6 fusion.32
  118.7 2.0 fusion.43
  120.7 5.6 %copy.62 = bf16[12,384,2,64]{3,2,0,1:T(2,128)(2,1)S(1)} copy(bf16[12,384,2,64]{1,3,2,0:T(8,128)(2,1)} %fusion.43) | data formatting | bytes 2359296 | tf_op jit(solution)/shard_map/convert_element_type | solution.py:139
  126.3 2.2 reshape.193
  128.6 6.4 %all-to-all-start.2 = ((bf16[32,2,9216]{2,1,0:T(2,128)(2,1)}), bf16[32,2,9216]{2,1,0:T(2,128)(2,1)S(1)}, u32[]{:S(2)}, u32[]{:S(2)}) async-start(bf16[32,2,9216]{2,1,0:T(2,128)(2,1)} %reshape.193), calls=%async_computation.2 | async-start | bytes 2359296 | tf_op jit(solution)/shard_map/all_to_all | solution.py:140
  135.0 0.6 copy_bitcast_fusion.6
  135.6 0.6 copy_bitcast_fusion.8
  136.2 0.6 copy_bitcast_fusion.10
  136.9 0.6 copy_bitcast_fusion.12
  137.5 0.6 copy_bitcast_fusion.14
  138.1 0.6 copy_bitcast_fusion.16
  138.7 2.1 fusion.97
  140.8 0.6 copy_bitcast_fusion.18
  141.4 0.6 copy_bitcast_fusion.20
  142.0 6.0 %fusion.71 = (f32[1,384,768]{2,1,0:T(8,128)}, f32[1,384,768]{2,1,0:T(8,128)}) fusion(f32[384]{0:T(512)S(1)} %copy-done.46, f32[384]{0:T(512)S(1)} %copy-done.47), kind=kLoop, calls=%fused_computation.86 | loop fusion | flops 3244032 | bytes 2362368 | tf_op jit(solution)/shard_map/mul | solution.py:44
  148.0 17.5 %all-to-all-done.2 = bf16[32,2,9216]{2,1,0:T(2,128)(2,1)S(1)} async-done(((bf16[32,2,9216]{2,1,0:T(2,128)(2,1)}), bf16[32,2,9216]{2,1,0:T(2,128)(2,1)S(1)}, u32[]{:S(2)}, u32[]{:S(2)}) %all-to-all-start.2) | async-done | bytes 1179680 | tf_op jit(solution)/shard_map/all_to_all | solution.py:140
  165.5 1.4 reshape.194
  166.9 3.0 %copy.64 = bf16[32,12,12,2,64]{4,3,2,1,0:T(2,128)(2,1)} copy(bf16[32,12,12,2,64]{4,3,1,2,0:T(2,128)(2,1)S(1)} %bitcast.150) | data formatting | bytes 2359296 | tf_op jit(solution)/shard_map/all_to_all | solution.py:140
  169.9 5.9 %copy.65 = bf16[384,12,2,64]{0,3,2,1:T(8,128)(2,1)S(1)} copy(bf16[384,12,2,64]{3,2,1,0:T(2,128)(2,1)} %bitcast.151) | data formatting | bytes 2359296 | tf_op jit(solution)/shard_map/all_to_all | solution.py:140
  175.8 1.1 fusion.50
  177.1 1.2 fusion.42
  178.7 6.3 %collective-permute-start = (bf16[2,772,64]{1,2,0:T(8,128)(2,1)S(1)}, bf16[2,772,64]{1,2,0:T(8,128)(2,1)S(1)}, u32[]{:S(2)}, u32[]{:S(2)}) collective-permute-start(bf16[2,772,64]{1,2,0:T(8,128)(2,1)S(1)} %get-tuple-element.12), channel_id=1, source_target_pairs={{0,8},{8,16},{16,24},{24,32},{32,40},{40,48},{48,56},{56,64},{64,7... | collective-permute-start | bytes 592904 | tf_op jit(solution)/shard_map/ppermute | solution.py:21
  185.0 1.9 collective-permute-start.1
  187.1 0.8 collective-permute-done
  187.9 4.4 %collective-permute-done.1 = bf16[2,772,64]{1,2,0:T(8,128)(2,1)S(1)} collective-permute-done((bf16[2,772,64]{1,2,0:T(8,128)(2,1)S(1)}, bf16[2,772,64]{1,2,0:T(8,128)(2,1)S(1)}, u32[]{:S(2)}, u32[]{:S(2)}) %collective-permute-start.1) | collective-permute-done | bytes 197664 | tf_op jit(solution)/shard_map/ppermute | solution.py:24
  192.3 2.0 maximum_maximum_fusion
  194.5 15.5 %fusion.29 = bf16[12,768,64]{1,2,0:T(8,128)(2,1)} fusion(bf16[12,768,64]{1,2,0:T(8,128)(2,1)S(1)} %fusion.42, bf16[12,2,64]{1,2,0:T(8,128)(2,1)S(1)} %get-tuple-element.15, bf16[12,2,64]{1,2,0:T(8,128)(2,1)S(1)} %get-tuple-element.14, bf16[14,772,64]{1,2,0:T(8,128)(2,1)S(1)} %get-tuple-element.11, bf16[14,772,64]{1,2,0:T(8,128)(2,1)S(1)} %get-tuple-element.10, ...), kind=kLoop, calls=%fused_computation.42 | loop fusion | flops 51904512 | bytes 26035200 | tf_op jit(solution)/shard_map/convert_element_type | solution.py:151
  210.0 3.9 %copy.67 = bf16[12,768,64]{2,0,1:T(8,128)(2,1)S(1)} copy(bf16[12,768,64]{1,2,0:T(8,128)(2,1)} %fusion.29) | data formatting | bytes 2359296 | tf_op jit(solution)/shard_map/convert_element_type | solution.py:151
  213.9 2.9 %reshape.195 = bf16[8,2,36864]{2,1,0:T(2,128)(2,1)} reshape(bf16[768,12,64]{2,1,0:T(8,128)(2,1)S(1)} %bitcast.147) | data formatting | bytes 2359296
  216.8 19.3 %all_to_all.72 = bf16[8,2,36864]{2,1,0:T(2,128)(2,1)S(1)} all-to-all(bf16[8,2,36864]{2,1,0:T(2,128)(2,1)} %reshape.195), channel_id=1, replica_groups=mesh['lat'=32,'lon'=8] {'lon'}, dimensions={0} | all-to-all | bytes 2359296 | tf_op jit(solution)/shard_map/all_to_all | solution.py:152
  236.2 3.2 %reshape.196 = bf16[768,12,64]{2,1,0:T(8,128)(2,1)} reshape(bf16[8,2,36864]{2,1,0:T(2,128)(2,1)S(1)} %all_to_all.72) | data formatting | bytes 2359296
  239.3 3.9 %copy.68 = bf16[12,8,96,64]{2,3,1,0:T(8,128)(2,1)S(1)} copy(bf16[12,8,96,64]{3,0,2,1:T(8,128)(2,1)} %bitcast.146) | data formatting | bytes 2359296 | tf_op jit(solution)/shard_map/all_to_all | solution.py:152
  243.2 2.1 bitcast_convert_fusion
  245.6 0.5 multiply_reduce_fusion
  246.2 5.7 %copy.69 = f32[12,96,8,64]{1,0,3,2:T(8,128)} copy(f32[12,96,8,64]{1,3,2,0:T(8,128)} %bitcast_convert_fusion) | data formatting | bytes 4718592 | tf_op jit(solution)/shard_map/convert_element_type | solution.py:73
  251.9 5.1 %reshape.179 = f32[1152,512]{0,1:T(8,128)} reshape(f32[12,96,8,64]{1,0,3,2:T(8,128)} %copy.69) | data formatting | bytes 4718592 | tf_op jit(solution)/shard_map/convert_element_type | solution.py:73
  257.1 1.5 copy.70
  258.6 7.2 %fusion.13 = bf16[1152,512]{1,0:T(8,128)(2,1)} fusion(bf16[1024,512]{1,0:T(8,128)(2,1)} %param.26, bf16[1152,512]{1,0:T(8,128)(2,1)} %bitcast.153, f32[512]{0:T(512)} %param.27, bf16[512,1024]{1,0:T(8,128)(2,1)} %param.24, f32[1024]{0:T(1024)} %param.25, f32[1152,512]{0,1:T(8,128)} %reshape.179, f32[512]{0:T(512)} %param.23, f32[1152]{0:T(1024)S(1)} %rsqrt.12, ...), kind=kOutput, calls=%fused_computation.17 | convolution fusion | flops 2432434176 | bytes 6833152 | tf_op jit(solution)/shard_map/dot_general | solution.py:79
  (111 shorter events, 1.6 us)
Async XLA Ops:
  0.6 116.0 %copy-start = (bf16[12,384,384]{2,1,0:T(8,128)(2,1)S(1)}, bf16[12,384,384]{2,1,0:T(8,128)(2,1)}, u32[]{:S(2)}) copy-start(bf16[12,384,384]{2,1,0:T(8,128)(2,1)} %param.16) | copy-start | bytes 10616836
  5.1 33.1 %all-to-all-start = ((bf16[12,96,512]{1,0,2:T(8,128)(2,1)}), bf16[12,96,512]{1,0,2:T(8,128)(2,1)}, u32[]{:S(2)}, u32[]{:S(2)}) async-start(bf16[12,96,512]{1,0,2:T(8,128)(2,1)} %copy.55), calls=%async_computation | async-start | bytes 4194304 | tf_op jit(solution)/shard_map/all_to_all | solution.py:110
  45.8 3.3 %copy-start.5 = (f32[1,384,768]{2,1,0:T(8,128)S(1)}, f32[1,384,768]{2,1,0:T(8,128)}, u32[]{:S(2)}) copy-start(f32[1,384,768]{2,1,0:T(8,128)} %get-tuple-element.41) | copy-start | bytes 3538948
  45.8 3.3 %copy-start.6 = (f32[1,384,768]{2,1,0:T(8,128)S(1)}, f32[1,384,768]{2,1,0:T(8,128)}, u32[]{:S(2)}) copy-start(f32[1,384,768]{2,1,0:T(8,128)} %get-tuple-element.42) | copy-start | bytes 3538948
  45.8 3.3 %copy-start.7 = (bf16[12,768,64,1]{1,2,0,3:T(8,128)(2,1)S(1)}, bf16[12,768,64,1]{1,2,0,3:T(8,128)(2,1)}, u32[]{:S(2)}) copy-start(bf16[12,768,64,1]{1,2,0,3:T(8,128)(2,1)} %reshape.182) | copy-start | bytes 3538948
  45.8 3.3 %copy-start.50 = (f32[12]{0:T(128)S(1)}, f32[12]{0:T(128)}, u32[]{:S(2)}) copy-start(f32[12]{0:T(128)} %param.15) | copy-start | bytes 148
  64.2 17.3 %copy-start.48 = (f32[12,12]{1,0:T(8,128)S(1)}, f32[12,12]{1,0:T(8,128)}, u32[]{:S(2)}) copy-start(f32[12,12]{1,0:T(8,128)} %param.21) | copy-start | bytes 1732
  64.2 17.3 %copy-start.49 = (s32[12,12]{1,0:T(8,128)S(1)}, s32[12,12]{1,0:T(8,128)}, u32[]{:S(2)}) copy-start(s32[12,12]{1,0:T(8,128)} %param.19) | copy-start | bytes 1732
  64.2 42.5 %all-to-all-start.1 = ((bf16[32,2,9216]{2,1,0:T(2,128)(2,1)}), bf16[32,2,9216]{2,1,0:T(2,128)(2,1)}, u32[]{:S(2)}, u32[]{:S(2)}) async-start(bf16[32,2,9216]{2,1,0:T(2,128)(2,1)} %reshape.191), calls=%async_computation.1 | async-start | bytes 2359296 | tf_op jit(solution)/shard_map/all_to_all | solution.py:122
  83.7 0.7 copy-start.8
  116.7 1.7 copy-start.9
  116.7 1.7 copy-start.10
  128.5 6.5 %copy-start.44 = (f32[12,1,64]{2,1,0:T(1,128)S(1)}, f32[12,1,64]{2,1,0:T(1,128)}, u32[]{:S(2)}) copy-start(f32[12,1,64]{2,1,0:T(1,128)} %get-tuple-element.23) | copy-start | bytes 9220
  128.5 6.5 %copy-start.45 = (f32[12,1,64]{2,1,0:T(1,128)S(1)}, f32[12,1,64]{2,1,0:T(1,128)}, u32[]{:S(2)}) copy-start(f32[12,1,64]{2,1,0:T(1,128)} %get-tuple-element.24) | copy-start | bytes 9220
  128.5 7.1 %copy-start.42 = (f32[12,1,64]{2,1,0:T(1,128)S(1)}, f32[12,1,64]{2,1,0:T(1,128)}, u32[]{:S(2)}) copy-start(f32[12,1,64]{2,1,0:T(1,128)} %get-tuple-element.25) | copy-start | bytes 9220
  128.5 7.1 %copy-start.43 = (f32[12,1,64]{2,1,0:T(1,128)S(1)}, f32[12,1,64]{2,1,0:T(1,128)}, u32[]{:S(2)}) copy-start(f32[12,1,64]{2,1,0:T(1,128)} %get-tuple-element.26) | copy-start | bytes 9220
  128.5 7.7 %copy-start.40 = (f32[12,1,64]{2,1,0:T(1,128)S(1)}, f32[12,1,64]{2,1,0:T(1,128)}, u32[]{:S(2)}) copy-start(f32[12,1,64]{2,1,0:T(1,128)} %get-tuple-element.27) | copy-start | bytes 9220
  128.5 7.7 %copy-start.41 = (f32[12,1,64]{2,1,0:T(1,128)S(1)}, f32[12,1,64]{2,1,0:T(1,128)}, u32[]{:S(2)}) copy-start(f32[12,1,64]{2,1,0:T(1,128)} %get-tuple-element.28) | copy-start | bytes 9220
  128.5 8.3 %copy-start.38 = (f32[12,1,64]{2,1,0:T(1,128)S(1)}, f32[12,1,64]{2,1,0:T(1,128)}, u32[]{:S(2)}) copy-start(f32[12,1,64]{2,1,0:T(1,128)} %get-tuple-element.29) | copy-start | bytes 9220
  128.6 8.3 %copy-start.39 = (f32[12,1,64]{2,1,0:T(1,128)S(1)}, f32[12,1,64]{2,1,0:T(1,128)}, u32[]{:S(2)}) copy-start(f32[12,1,64]{2,1,0:T(1,128)} %get-tuple-element.30) | copy-start | bytes 9220
  128.6 8.9 %copy-start.36 = (f32[12,1,64]{2,1,0:T(1,128)S(1)}, f32[12,1,64]{2,1,0:T(1,128)}, u32[]{:S(2)}) copy-start(f32[12,1,64]{2,1,0:T(1,128)} %get-tuple-element.31) | copy-start | bytes 9220
  128.6 8.9 %copy-start.37 = (f32[12,1,64]{2,1,0:T(1,128)S(1)}, f32[12,1,64]{2,1,0:T(1,128)}, u32[]{:S(2)}) copy-start(f32[12,1,64]{2,1,0:T(1,128)} %get-tuple-element.32) | copy-start | bytes 9220
  128.6 9.5 %copy-start.34 = (f32[12,1,64]{2,1,0:T(1,128)S(1)}, f32[12,1,64]{2,1,0:T(1,128)}, u32[]{:S(2)}) copy-start(f32[12,1,64]{2,1,0:T(1,128)} %get-tuple-element.33) | copy-start | bytes 9220
  128.6 9.5 %copy-start.35 = (f32[12,1,64]{2,1,0:T(1,128)S(1)}, f32[12,1,64]{2,1,0:T(1,128)}, u32[]{:S(2)}) copy-start(f32[12,1,64]{2,1,0:T(1,128)} %get-tuple-element.34) | copy-start | bytes 9220
  128.6 13.4 %copy-start.46 = (f32[384]{0:T(512)S(1)}, f32[384]{0:T(512)}, u32[]{:S(2)}) copy-start(f32[384]{0:T(512)} %select_multiply_fusion) | copy-start | bytes 4612
  128.6 13.4 %copy-start.47 = (f32[384]{0:T(512)S(1)}, f32[384]{0:T(512)}, u32[]{:S(2)}) copy-start(f32[384]{0:T(512)} %fusion.83) | copy-start | bytes 4612
  128.6 36.9 %all-to-all-start.2 = ((bf16[32,2,9216]{2,1,0:T(2,128)(2,1)}), bf16[32,2,9216]{2,1,0:T(2,128)(2,1)S(1)}, u32[]{:S(2)}, u32[]{:S(2)}) async-start(bf16[32,2,9216]{2,1,0:T(2,128)(2,1)} %reshape.193), calls=%async_computation.2 | async-start | bytes 2359296 | tf_op jit(solution)/shard_map/all_to_all | solution.py:140
  169.9 5.9 %copy-start.2 = (f32[1,384,768]{2,1,0:T(8,128)S(1)}, f32[1,384,768]{2,1,0:T(8,128)}, u32[]{:S(2)}) copy-start(f32[1,384,768]{2,1,0:T(8,128)} %get-tuple-element.45) | copy-start | bytes 3538948
  169.9 5.9 %copy-start.3 = (f32[1,384,768]{2,1,0:T(8,128)S(1)}, f32[1,384,768]{2,1,0:T(8,128)}, u32[]{:S(2)}) copy-start(f32[1,384,768]{2,1,0:T(8,128)} %get-tuple-element.46) | copy-start | bytes 3538948
  175.8 1.3 copy-start.4
  178.2 8.7 %copy-start.32 = (f32[12,1,64]{2,1,0:T(1,128)S(1)}, f32[12,1,64]{2,1,0:T(1,128)}, u32[]{:S(2)}) copy-start(f32[12,1,64]{2,1,0:T(1,128)} %get-tuple-element.35) | copy-start | bytes 9220
  178.2 8.7 %copy-start.33 = (f32[12,1,64]{2,1,0:T(1,128)S(1)}, f32[12,1,64]{2,1,0:T(1,128)}, u32[]{:S(2)}) copy-start(f32[12,1,64]{2,1,0:T(1,128)} %get-tuple-element.40) | copy-start | bytes 9220
  178.7 9.3 %collective-permute-start = (bf16[2,772,64]{1,2,0:T(8,128)(2,1)S(1)}, bf16[2,772,64]{1,2,0:T(8,128)(2,1)S(1)}, u32[]{:S(2)}, u32[]{:S(2)}) collective-permute-start(bf16[2,772,64]{1,2,0:T(8,128)(2,1)S(1)} %get-tuple-element.12), channel_id=1, source_target_pairs={{0,8},{8,16},{16,24},{24,32},{32,40},{40,48},{48,56},{56,64},{64,7... | collective-permute-start | bytes 592904 | tf_op jit(solution)/shard_map/ppermute | solution.py:21
  185.0 7.3 %collective-permute-start.1 = (bf16[2,772,64]{1,2,0:T(8,128)(2,1)S(1)}, bf16[2,772,64]{1,2,0:T(8,128)(2,1)S(1)}, u32[]{:S(2)}, u32[]{:S(2)}) collective-permute-start(bf16[2,772,64]{1,2,0:T(8,128)(2,1)S(1)} %get-tuple-element.13), channel_id=1, source_target_pairs={{8,0},{16,8},{24,16},{32,24},{40,32},{48,40},{56,48},{64,56},{72,6... | collective-permute-start | bytes 592904 | tf_op jit(solution)/shard_map/ppermute | solution.py:24
  186.9 7.4 %copy-start.11 = (f32[12,64]{1,0:T(8,128)S(1)}, f32[12,64]{1,0:T(8,128)}, u32[]{:S(2)}) copy-start(f32[12,64]{1,0:T(8,128)} %get-tuple-element.49) | copy-start | bytes 9220
  186.9 7.4 %copy-start.12 = (f32[12,64]{1,0:T(8,128)S(1)}, f32[12,64]{1,0:T(8,128)}, u32[]{:S(2)}) copy-start(f32[12,64]{1,0:T(8,128)} %get-tuple-element.50) | copy-start | bytes 9220
  186.9 7.4 %copy-start.13 = (f32[12,64]{1,0:T(8,128)S(1)}, f32[12,64]{1,0:T(8,128)}, u32[]{:S(2)}) copy-start(f32[12,64]{1,0:T(8,128)} %get-tuple-element.51) | copy-start | bytes 9220
  187.0 7.4 %copy-start.14 = (f32[12,64]{1,0:T(8,128)S(1)}, f32[12,64]{1,0:T(8,128)}, u32[]{:S(2)}) copy-start(f32[12,64]{1,0:T(8,128)} %get-tuple-element.52) | copy-start | bytes 9220
  187.0 7.4 %copy-start.15 = (f32[12,64]{1,0:T(8,128)S(1)}, f32[12,64]{1,0:T(8,128)}, u32[]{:S(2)}) copy-start(f32[12,64]{1,0:T(8,128)} %get-tuple-element.53) | copy-start | bytes 9220
  187.0 7.4 %copy-start.16 = (f32[12,64]{1,0:T(8,128)S(1)}, f32[12,64]{1,0:T(8,128)}, u32[]{:S(2)}) copy-start(f32[12,64]{1,0:T(8,128)} %get-tuple-element.54) | copy-start | bytes 9220
  187.0 7.4 %copy-start.17 = (f32[12,64]{1,0:T(8,128)S(1)}, f32[12,64]{1,0:T(8,128)}, u32[]{:S(2)}) copy-start(f32[12,64]{1,0:T(8,128)} %get-tuple-element.55) | copy-start | bytes 9220
  187.0 7.4 %copy-start.18 = (f32[12,64]{1,0:T(8,128)S(1)}, f32[12,64]{1,0:T(8,128)}, u32[]{:S(2)}) copy-start(f32[12,64]{1,0:T(8,128)} %get-tuple-element.56) | copy-start | bytes 9220
  187.0 7.4 %copy-start.19 = (f32[12,64]{1,0:T(8,128)S(1)}, f32[12,64]{1,0:T(8,128)}, u32[]{:S(2)}) copy-start(f32[12,64]{1,0:T(8,128)} %get-tuple-element.57) | copy-start | bytes 9220
  187.0 7.4 %copy-start.20 = (f32[12,64]{1,0:T(8,128)S(1)}, f32[12,64]{1,0:T(8,128)}, u32[]{:S(2)}) copy-start(f32[12,64]{1,0:T(8,128)} %get-tuple-element.58) | copy-start | bytes 9220
  187.0 7.4 %copy-start.21 = (f32[12,64]{1,0:T(8,128)S(1)}, f32[12,64]{1,0:T(8,128)}, u32[]{:S(2)}) copy-start(f32[12,64]{1,0:T(8,128)} %get-tuple-element.59) | copy-start | bytes 9220
  187.0 7.4 %copy-start.22 = (f32[12,64]{1,0:T(8,128)S(1)}, f32[12,64]{1,0:T(8,128)}, u32[]{:S(2)}) copy-start(f32[12,64]{1,0:T(8,128)} %get-tuple-element.60) | copy-start | bytes 9220
  187.0 7.4 %copy-start.23 = (f32[12,64]{1,0:T(8,128)S(1)}, f32[12,64]{1,0:T(8,128)}, u32[]{:S(2)}) copy-start(f32[12,64]{1,0:T(8,128)} %get-tuple-element.61) | copy-start | bytes 9220
  187.1 7.4 %copy-start.24 = (f32[12,64]{1,0:T(8,128)S(1)}, f32[12,64]{1,0:T(8,128)}, u32[]{:S(2)}) copy-start(f32[12,64]{1,0:T(8,128)} %get-tuple-element.62) | copy-start | bytes 9220
  187.1 7.4 %copy-start.25 = (f32[12,64]{1,0:T(8,128)S(1)}, f32[12,64]{1,0:T(8,128)}, u32[]{:S(2)}) copy-start(f32[12,64]{1,0:T(8,128)} %get-tuple-element.63) | copy-start | bytes 9220
  187.1 7.4 %copy-start.26 = (f32[12,64]{1,0:T(8,128)S(1)}, f32[12,64]{1,0:T(8,128)}, u32[]{:S(2)}) copy-start(f32[12,64]{1,0:T(8,128)} %get-tuple-element.64) | copy-start | bytes 9220
  187.1 7.4 %copy-start.27 = (f32[12,64]{1,0:T(8,128)S(1)}, f32[12,64]{1,0:T(8,128)}, u32[]{:S(2)}) copy-start(f32[12,64]{1,0:T(8,128)} %get-tuple-element.65) | copy-start | bytes 9220
  187.1 7.4 %copy-start.28 = (f32[12,64]{1,0:T(8,128)S(1)}, f32[12,64]{1,0:T(8,128)}, u32[]{:S(2)}) copy-start(f32[12,64]{1,0:T(8,128)} %get-tuple-element.66) | copy-start | bytes 9220
  187.1 7.4 %copy-start.29 = (f32[12,64]{1,0:T(8,128)S(1)}, f32[12,64]{1,0:T(8,128)}, u32[]{:S(2)}) copy-start(f32[12,64]{1,0:T(8,128)} %get-tuple-element.67) | copy-start | bytes 9220
  187.1 7.4 %copy-start.30 = (f32[12,64]{1,0:T(8,128)S(1)}, f32[12,64]{1,0:T(8,128)}, u32[]{:S(2)}) copy-start(f32[12,64]{1,0:T(8,128)} %get-tuple-element.68) | copy-start | bytes 9220
  187.1 7.4 %copy-start.31 = (f32[12,1,64]{2,0,1:T(8,128)S(1)}, f32[12,1,64]{2,0,1:T(8,128)}, u32[]{:S(2)}) copy-start(f32[12,1,64]{2,0,1:T(8,128)} %copy.132) | copy-start | bytes 9220
  258.6 7.2 %copy-start.1 = (bf16[12,384,384]{2,1,0:T(8,128)(2,1)S(1)}, bf16[12,384,384]{2,1,0:T(8,128)(2,1)}, u32[]{:S(2)}) copy-start(bf16[12,384,384]{2,1,0:T(8,128)(2,1)} %param.16) | copy-start | bytes 10616836
where the time goes:
time: 268 us; the launch traced here: 266 us
  local copies, waits for them, and re-layouts  95.1 us (35%)
  waiting for transfers between devices  62.2 us (23%)
  other arithmetic  34.5 us (13%)
  starting transfers between devices  32.4 us (12%)
  matrix products  20.8 us (8%)
  blocking collectives  19.3 us (7%)
    unnamed x123, local copies, waits for them, and re-layouts  35.8 us
    all_to_all x1, waiting for transfers between devices, shards(): lax.all_to_all(field, 'lon', split_axis=2, concat_axis=1, tiled=True)  20.8 us
    all_to_all x1, blocking collectives, shards(): lax.all_to_all(spatial_part, 'lon', split_axis=1, concat_axis=2, tiled=True)  19.3 us
    all_to_all x1, waiting for transfers between devices, shards(): lax.all_to_all(weighted, 'lat', split_axis=0, concat_axis=1, tiled=True)  18.7 us
    all_to_all x1, waiting for transfers between devices, shards(): lax.all_to_all(synthesis, 'lat', split_axis=1, concat_axis=0, tiled=True)  17.5 us
    convert_element_type x1, other arithmetic, shards(): spatial_part = (wave.astype(jnp.float32) + conv).astype(jnp.bfloat16)  15.5 us
    all_to_all x1, starting transfers between devices, shards(): lax.all_to_all(weighted, 'lat', split_axis=0, concat_axis=1, tiled=True)  11.9 us
    convert_element_type x2, local copies, waits for them, and re-layouts, channel_mlp(): tokens = spatial.reshape(-1, channels).astype(jnp.float32)  10.8 us
  transfers between devices with their start and end apart: 5, of which 5 were waited for; matrix products, arithmetic and copies ran while one was open for 11% of the time, Pallas kernels for 0%

commit v1 on v0

v1 whole, which is shorter than its diff:
```python
import functools
import math

import jax
import jax.numpy as jnp
import ml_dtypes
import numpy as np
from jax import lax
from jax.experimental import pallas as pl
from jax.experimental.pallas import tpu as pltpu
from jax.sharding import PartitionSpec as P

HALO = 2
LANES = 128
MESH = pl.DeviceIdType.MESH
BF16 = jnp.bfloat16
F32 = jnp.float32


def tables(nlon, mmax, groups, blocks):
    per = mmax // groups
    waves = np.stack([np.arange(groups) * per + p for p in range(per)])
    waves = np.repeat(waves[:, None, :], 2, axis=1).reshape(-1)
    part = np.broadcast_to(np.array([0, 1])[None, :, None], (per, 2, groups)).reshape(-1)
    cols = nlon // blocks
    edge = np.array([-2, -1, cols, cols + 1])
    halo = (edge[:, None] + np.arange(blocks)[None, :] * cols).reshape(-1) % nlon
    points = np.concatenate([np.arange(nlon), halo])
    angle = (waves[:, None] * points[None, :] % nlon) * (2.0 * math.pi / nlon)
    wave = np.where(part[:, None] == 0, np.cos(angle), -np.sin(angle)) / math.sqrt(nlon)
    factor = np.where(waves == 0, 1.0, 2.0)
    forward = wave[:, :nlon].astype(ml_dtypes.bfloat16)
    inverse = (wave * factor[:, None]).T.astype(ml_dtypes.bfloat16)
    return forward, np.ascontiguousarray(inverse)


class Sizes:
    def __init__(self, mesh, lat_rows, lon_cols, channels, wave_block, degrees):
        self.ni = mesh.shape["lat"]
        self.nj = mesh.shape["lon"]
        self.nq = channels // LANES
        self.nh = self.nj // self.nq
        self.groups = self.ni * self.nh
        self.rows = lat_rows
        self.trow = lat_rows // self.nh
        self.cols = lon_cols
        self.nlon = lon_cols * self.nj
        self.chan = channels
        self.wper = wave_block // self.nh
        self.deg = degrees
        self.nlat = lat_rows * self.ni
        self.step = 2
        self.chunks = self.trow // self.step
        self.mr = 2 * self.wper
        self.blk = self.step * self.mr


def exchange_kernel(
    z,
    quad_ref,
    field_ref,
    leg_ref,
    fr_ref,
    fi_ref,
    fwd_ref,
    inv_ref,
    wave_out,
    edge_out,
    cols_in,
    ltab,
    ltrans,
    fwd,
    inv,
    gr,
    gi,
    stage,
    wide,
    send1,
    recv1,
    send2,
    recv2,
    wbuf,
    ebuf32,
    ebuf,
    load_sem,
    own_sem,
    a_send,
    a_recv,
    b_send,
    b_recv,
    c_send,
    c_recv,
    d_send,
    d_recv,
    e_send,
    e_recv,
    out_own,
    h_send,
    h_recv,
):
    i = lax.axis_index("lat")
    j = lax.axis_index("lon")
    h = j // z.nq
    q = j % z.nq
    me = i * z.nh + h
    lane0 = pl.multiple_of(q * LANES, LANES)
    G = z.groups

    loads = [
        pltpu.make_async_copy(leg_ref.at[pl.ds(h * z.wper, z.wper)], ltab, load_sem.at[0]),
        pltpu.make_async_copy(fwd_ref, fwd, load_sem.at[1]),
        pltpu.make_async_copy(inv_ref, inv, load_sem.at[2]),
        pltpu.make_async_copy(fr_ref.at[:, pl.ds(lane0, LANES)], gr, load_sem.at[3]),
        pltpu.make_async_copy(fi_ref.at[:, pl.ds(lane0, LANES)], gi, load_sem.at[4]),
    ]
    own = pltpu.make_async_copy(
        field_ref.at[pl.ds(h * z.trow, z.trow), :, pl.ds(lane0, LANES)],
        cols_in.at[:, pl.ds(pl.multiple_of(j * z.cols, 16), z.cols), :],
        own_sem,
    )
    loads[1].start()
    own.start()
    for k in (0, 2, 3, 4):
        loads[k].start()

    def group_peer(o):
        nz = max(G // 8, 1)
        a = (o % nz) * 3 % nz
        b = o // nz
        per = G // nz
        here = me // (per // 2) % nz if nz > 1 else 0
        half = me // (G // 2)
        low = me % (per // 2)
        zz = (here + a) % nz
        other = (half * (per // 2) + low + b) % per
        peer = (other // (per // 2)) * (G // 2) + zz * (per // 2) + other % (per // 2)
        return peer

    def group_id(peer):
        return {"lat": peer // z.nh, "lon": (peer % z.nh) * z.nq + q}

    barrier = pltpu.get_barrier_semaphore()

    def greet(o, carry):
        pl.semaphore_signal(
            barrier, inc=1, device_id=group_id(group_peer(o)), device_id_type=MESH
        )
        return carry

    def greet_lon(o, carry):
        hh = (h + o // (z.nq - 1)) % z.nh
        qq = (q + 1 + o % (z.nq - 1)) % z.nq
        pl.semaphore_signal(
            barrier, inc=1, device_id={"lat": i, "lon": hh * z.nq + qq}, device_id_type=MESH
        )
        return carry

    lon_only = z.nh * (z.nq - 1)
    lax.fori_loop(0, lon_only, greet_lon, 0)
    lax.fori_loop(1, G, greet, 0)
    pl.semaphore_wait(barrier, lon_only + G - 1)

    for c in range(z.chunks):

        def send_a(o, carry):
            p = (j + o) % z.nj
            hp = p // z.nq
            qp = p % z.nq
            pltpu.make_async_remote_copy(
                src_ref=field_ref.at[
                    pl.ds(hp * z.trow + c * z.step, z.step),
                    :,
                    pl.ds(pl.multiple_of(qp * LANES, LANES), LANES),
                ],
                dst_ref=cols_in.at[
                    pl.ds(c * z.step, z.step), pl.ds(pl.multiple_of(j * z.cols, 16), z.cols), :
                ],
                send_sem=a_send,
                recv_sem=a_recv.at[c],
                device_id={"lat": i, "lon": p},
                device_id_type=MESH,
            ).start()
            return carry

        lax.fori_loop(1, z.nj, send_a, 0)

    loads[0].wait()
    for w in range(z.wper):
        ltrans[w] = ltab[w].T
    loads[1].wait()
    own.wait()

    def await_bytes(ref, sem):
        pltpu.make_async_copy(ref, ref, sem).wait()

    def pack_and_send(c, send, recv, send_sem, recv_sem, load_block):
        def pack(s, carry):
            send[c, s] = load_block(s).astype(BF16)
            return carry

        lax.fori_loop(0, G, pack, 0, unroll=8)
        recv[c, me] = send[c, me]

        def start(o, carry):
            peer = group_peer(o)
            pltpu.make_async_remote_copy(
                src_ref=send.at[c, peer],
                dst_ref=recv.at[c, me],
                send_sem=send_sem,
                recv_sem=recv_sem.at[c],
                device_id=group_id(peer),
                device_id_type=MESH,
            ).start()
            return carry

        lax.fori_loop(1, G, start, 0)

    for c in range(z.chunks):
        span = z.cols * (z.nj - 1)
        await_bytes(cols_in.at[pl.ds(c * z.step, z.step), pl.ds(0, span), :], a_recv.at[c])
        rhs = jnp.concatenate([cols_in[c * z.step + k] for k in range(z.step)], axis=1)
        spec = jnp.dot(fwd[...], rhs, preferred_element_type=F32)
        for k in range(z.step):
            quad = quad_ref[h * z.trow + c * z.step + k]
            part = spec[:, k * LANES : (k + 1) * LANES] * quad
            for p in range(z.mr):
                stage[pl.ds(k * z.mr + p, G, stride=z.blk), :] = part[p * G : (p + 1) * G]
        pack_and_send(
            c,
            send1,
            recv1,
            b_send,
            b_recv,
            lambda s: stage[pl.ds(pl.multiple_of(s * z.blk, 8), z.blk), :],
        )

    for c in range(z.chunks):
        await_bytes(recv1.at[c, pl.ds(0, G - 1)], b_recv.at[c])

        def unpack(s, carry):
            at = pl.multiple_of(s * (z.blk * z.chunks) + c * z.blk, 8)
            wide[pl.ds(at, z.blk), :] = recv1[c, s].astype(F32)
            return carry

        lax.fori_loop(0, G, unpack, 0, unroll=8)

    for k in (2, 3, 4):
        loads[k].wait()

    for w in range(z.wper):
        weighted = jnp.concatenate(
            [wide[pl.ds(2 * w + r, z.nlat, stride=z.mr), :] for r in range(2)], axis=1
        ).astype(BF16)
        coef = jnp.dot(ltab[w], weighted, preferred_element_type=F32)
        re = coef[:, :LANES]
        im = coef[:, LANES:]
        a = gr[...]
        b = gi[...]
        filt = jnp.concatenate([a * re - b * im, a * im + b * re], axis=1).astype(BF16)
        syn = jnp.dot(ltrans[w], filt, preferred_element_type=F32)
        for r in range(2):
            wide[pl.ds(2 * w + r, z.nlat, stride=z.mr), :] = syn[:, r * LANES : (r + 1) * LANES]

    for c in range(z.chunks):
        pack_and_send(
            c,
            send2,
            recv2,
            c_send,
            c_recv,
            lambda s: wide[
                pl.ds(pl.multiple_of(s * (z.blk * z.chunks) + c * z.blk, 8), z.blk), :
            ],
        )

    own_copies = []
    for c in range(z.chunks):
        await_bytes(recv2.at[c, pl.ds(0, G - 1)], c_recv.at[c])

        def unpack(s, carry):
            stage[pl.ds(pl.multiple_of(s * z.blk, 8), z.blk), :] = recv2[c, s].astype(F32)
            return carry

        lax.fori_loop(0, G, unpack, 0, unroll=8)
        modes = jnp.concatenate(
            [
                jnp.concatenate(
                    [stage[pl.ds(k * z.mr + p, G, stride=z.blk), :] for p in range(z.mr)],
                    axis=0,
                )
                for k in range(z.step)
            ],
            axis=1,
        ).astype(BF16)
        full = jnp.dot(inv[...], modes, preferred_element_type=F32)
        edge_rows = 4 * z.step
        for k in range(z.step):
            half = full[:, k * LANES : (k + 1) * LANES]
            wbuf[c * z.step + k] = half[: z.nlon].astype(BF16)
            for e in range(4):
                at = z.nlon + e * z.nj
                ebuf32[pl.ds(k * 4 + e, z.nj, stride=edge_rows), :] = half[at : at + z.nj]
        for p in range(z.nj):
            ebuf[c, p] = ebuf32[p * edge_rows : (p + 1) * edge_rows, :].astype(BF16).astype(F32)

        row = HALO + h * z.trow + c * z.step

        def wave_pair(p):
            return (
                wbuf.at[
                    pl.ds(c * z.step, z.step), pl.ds(pl.multiple_of(p * z.cols, 16), z.cols), :
                ],
                wave_out.at[pl.ds(row, z.step), :, pl.ds(lane0, LANES)],
            )

        def edge_pair(p):
            return (
                ebuf.at[c, p],
                edge_out.at[
                    pl.ds(pl.multiple_of(row * 4, 8), edge_rows), pl.ds(lane0, LANES)
                ],
            )

        def send_d(o, carry):
            p = (j + o) % z.nj
            for (src, dst), ss, rs in (
                (wave_pair(p), d_send, d_recv.at[c]),
                (edge_pair(p), e_send, e_recv.at[c]),
            ):
                pltpu.make_async_remote_copy(
                    src_ref=src,
                    dst_ref=dst,
                    send_sem=ss,
                    recv_sem=rs,
                    device_id={"lat": i, "lon": p},
                    device_id_type=MESH,
                ).start()
            return carry

        lax.fori_loop(1, z.nj, send_d, 0)
        for n, (src, dst) in enumerate((wave_pair(j), edge_pair(j))):
            copy = pltpu.make_async_copy(src, dst, out_own.at[c, n])
            copy.start()
            own_copies.append(copy)

    for copy in own_copies:
        copy.wait()
    for c in range(z.chunks):
        span = z.cols * (z.nj - 1)
        await_bytes(wbuf.at[pl.ds(c * z.step, z.step), pl.ds(0, span), :], d_recv.at[c])
        await_bytes(ebuf.at[c, pl.ds(0, z.nj - 1)], e_recv.at[c])

    last = z.rows + HALO
    moves = []
    for n, (src_row, dst_row, to) in enumerate(
        ((HALO, last, (i + z.ni - 1) % z.ni), (last - HALO, 0, (i + 1) % z.ni))
    ):
        for f, (src, dst) in enumerate(
            (
                (wave_out.at[pl.ds(src_row, HALO)], wave_out.at[pl.ds(dst_row, HALO)]),
                (
                    edge_out.at[pl.ds(src_row * 4, HALO * 4)],
                    edge_out.at[pl.ds(dst_row * 4, HALO * 4)],
                ),
            )
        ):
            move = pltpu.make_async_remote_copy(
                src_ref=src,
                dst_ref=dst,
                send_sem=h_send.at[n, f],
                recv_sem=h_recv.at[n, f],
                device_id={"lat": to, "lon": j},
                device_id_type=MESH,
            )
            move.start()
            moves.append(move)
    for move in moves:
        move.wait()

    span = z.cols * (z.nj - 1)
    await_bytes(wbuf.at[:, pl.ds(0, span), :], a_send)
    await_bytes(send1.at[:, pl.ds(0, G - 1)], b_send)
    await_bytes(send2.at[:, pl.ds(0, G - 1)], c_send)
    await_bytes(wbuf.at[:, pl.ds(0, span), :], d_send)
    await_bytes(ebuf.at[:, pl.ds(0, z.nj - 1)], e_send)


def exchange(z, field, quad, legendre, fr, fi, fwd, inv):
    hbm = pl.BlockSpec(memory_space=pl.ANY)
    dma = pltpu.SemaphoreType.DMA
    flat = z.groups * z.blk
    span = z.rows + 2 * HALO
    return pl.pallas_call(
        functools.partial(exchange_kernel, z),
        name="exchange",
        out_shape=(
            jax.ShapeDtypeStruct((span, z.cols, z.chan), BF16),
            jax.ShapeDtypeStruct((span * 4, z.chan), F32),
        ),
        in_specs=[pl.BlockSpec(memory_space=pltpu.SMEM)] + [hbm] * 6,
        out_specs=(hbm, hbm),
        scratch_shapes=[
            pltpu.VMEM((z.trow, z.nlon, LANES), BF16),
            pltpu.VMEM((z.wper, z.deg, z.nlat), BF16),
            pltpu.VMEM((z.wper, z.nlat, z.deg), BF16),
            pltpu.VMEM(fwd.shape, BF16),
            pltpu.VMEM(inv.shape, BF16),
            pltpu.VMEM((z.deg, LANES), F32),
            pltpu.VMEM((z.deg, LANES), F32),
            pltpu.VMEM((flat, LANES), F32),
            pltpu.VMEM((flat * z.chunks, LANES), F32),
            pltpu.VMEM((z.chunks, z.groups, z.blk, LANES), BF16),
            pltpu.VMEM((z.chunks, z.groups, z.blk, LANES), BF16),
            pltpu.VMEM((z.chunks, z.groups, z.blk, LANES), BF16),
            pltpu.VMEM((z.chunks, z.groups, z.blk, LANES), BF16),
            pltpu.VMEM((z.trow, z.nlon, LANES), BF16),
            pltpu.VMEM((z.nj * 4 * z.step, LANES), F32),
            pltpu.VMEM((z.chunks, z.nj, 4 * z.step, LANES), F32),
            dma((5,)),
            dma,
            dma,
            dma((z.chunks,)),
            dma,
            dma((z.chunks,)),
            dma,
            dma((z.chunks,)),
            dma,
            dma((z.chunks,)),
            dma,
            dma((z.chunks,)),
            dma((z.chunks, 2)),
            dma((2, 2)),
            dma((2, 2)),
        ],
        compiler_params=pltpu.CompilerParams(
            collective_id=0, has_side_effects=True, vmem_limit_bytes=60 << 20
        ),
        cost_estimate=pl.CostEstimate(
            flops=4 * z.trow * z.nlon * z.nlon * LANES, bytes_accessed=1 << 24, transcendentals=0
        ),
    )(quad, field, legendre, fr, fi, fwd, inv)


def local_kernel(
    z,
    rstep,
    neighbour,
    basis,
    quad,
    place,
    wave_ref,
    edge_ref,
    field_ref,
    weight_ref,
    gain_ref,
    win_ref,
    bin_ref,
    wout_ref,
    bout_ref,
    out_ref,
    spatial_ref,
    padded,
):
    g = pl.program_id(0)
    span = z.rows + 2 * HALO
    slots = neighbour.shape[1]

    @pl.when(g == 0)
    def _():
        def widen(pair, carry):
            for q in range(z.nq):
                lanes = slice(q * LANES, (q + 1) * LANES)
                edges = edge_ref[pl.ds(pl.multiple_of(pair * 8, 8), 8), lanes]
                for k in range(2):
                    t = pair * 2 + k
                    padded[t, q, 8 : 8 + z.cols, :] = wave_ref[t, :, lanes].astype(F32)
                    padded[t, q, 6:8, :] = edges[4 * k : 4 * k + 2]
                    padded[t, q, 8 + z.cols : 10 + z.cols, :] = edges[4 * k + 2 : 4 * k + 4]
            return carry

        lax.fori_loop(0, span // 2, widen, 0)

        @pl.when(place[0] == 0)
        def _():
            padded[:HALO] = jnp.zeros((HALO,) + padded.shape[1:], F32)

        @pl.when(place[0] == z.ni - 1)
        def _():
            padded[span - HALO :] = jnp.zeros((HALO,) + padded.shape[1:], F32)

    def conv_row(k, carry):
        t = g * rstep + k
        for q in range(z.nq):
            lanes = slice(q * LANES, (q + 1) * LANES)
            total = padded[t + HALO, q, 8 : 8 + z.cols, :]
            for s in range(slots):
                n = neighbour[t, s]
                coef = weight_ref[basis[t, s], :, lanes] * quad[t, s]
                total = total + coef * padded[t + n // 5, q, pl.ds(6 + n % 5, z.cols), :]
            spatial_ref[k, :, lanes] = total.astype(BF16)
        return carry

    lax.fori_loop(0, rstep, conv_row, 0)
    tokens = spatial_ref[...].reshape(rstep * z.cols, z.chan).astype(F32)
    center = jnp.mean(tokens, axis=1, keepdims=True)
    tokens = tokens - center
    spread = jnp.mean(tokens * tokens, axis=1, keepdims=True)
    normed = (tokens * lax.rsqrt(spread + 1e-05) * gain_ref[...]).astype(BF16)
    hidden = jnp.dot(normed, win_ref[...], preferred_element_type=F32) + bin_ref[...]
    hidden = jax.nn.gelu(hidden).astype(BF16)
    result = jnp.dot(hidden, wout_ref[...], preferred_element_type=F32)
    result = result + bout_ref[...] + field_ref[...].reshape(tokens.shape).astype(F32)
    out_ref[...] = result.astype(BF16).reshape(out_ref.shape)


def local(z, wave, edge, field, neighbour, basis, quad, weight, gain, w_in, b_in, w_out, b_out):
    rstep = 2
    smem = pl.BlockSpec(memory_space=pltpu.SMEM)
    rows = pl.BlockSpec((rstep, z.cols, z.chan), lambda g: (g, 0, 0))

    def whole(x):
        return pl.BlockSpec(x.shape, lambda g: (0,) * x.ndim)

    span = z.rows + 2 * HALO
    place = lax.axis_index("lat").astype(jnp.int32)[None]
    gain, b_in, b_out, weight = gain[None], b_in[None], b_out[None], weight[:, None, :]
    shape = jax.ShapeDtypeStruct(field.shape, BF16)
    return pl.pallas_call(
        functools.partial(local_kernel, z, rstep),
        name="local",
        grid=(z.rows // rstep,),
        out_shape=(shape, shape),
        in_specs=[smem] * 4
        + [whole(wave), whole(edge), rows]
        + [whole(x) for x in (weight, gain, w_in, b_in, w_out, b_out)],
        out_specs=(rows, rows),
        scratch_shapes=[pltpu.VMEM((span, z.nq, z.cols + 16, LANES), F32)],
        compiler_params=pltpu.CompilerParams(vmem_limit_bytes=48 << 20),
    )(
        neighbour,
        basis,
        quad,
        place,
        wave,
        edge,
        field,
        weight,
        gain,
        w_in,
        b_in,
        w_out,
        b_out,
    )


def shards(
    mesh,
    field,
    quad_weight,
    legendre,
    filter_real,
    filter_imag,
    neighbour,
    basis,
    disco_quad,
    disco_weight,
    norm_gain,
    w_in,
    b_in,
    w_out,
    b_out,
):
    lat_rows, lon_cols, channels = field.shape
    z = Sizes(mesh, lat_rows, lon_cols, channels, legendre.shape[0], legendre.shape[1])
    fwd, inv = tables(z.nlon, z.wper * z.groups, z.groups, z.nj)
    wave, edge = exchange(
        z, field, quad_weight, legendre, filter_real, filter_imag, jnp.asarray(fwd), jnp.asarray(inv)
    )
    return local(
        z,
        wave,
        edge,
        field,
        neighbour,
        basis,
        disco_quad,
        disco_weight,
        norm_gain,
        w_in,
        b_in,
        w_out,
        b_out,
    )


def solution(mesh):
    placed = (
        P("lat", "lon", None),
        P("lat"),
        P("lat", None, None),
        P(),
        P(),
        P("lat", None),
        P("lat", None),
        P("lat", None),
        P(),
        P(),
        P(),
        P(),
        P(),
        P(),
    )
    return jax.shard_map(
        functools.partial(shards, mesh),
        mesh=mesh,
        in_specs=placed,
        out_specs=(P("lat", "lon", None), P("lat", "lon", None)),
        check_vma=False,
    )
```

time: 268 us -> 114 us (0.43)
  Pallas kernels: 0 us -> 110 us
  local copies, waits for them, and re-layouts: 95.1 us -> 3.09 us
  waiting for transfers between devices: 62.2 us -> 0 us
  other arithmetic: 34.5 us -> 0 us
  starting transfers between devices: 32.4 us -> 0 us
  matrix products: 20.8 us -> 0 us
  blocking collectives: 19.3 us -> 0 us
    pallas_call x0 -> x2, Pallas kernels: none -> 110 us  [the longest x1 97.8 us: exchange(): pl.pallas_call(functools.partial(exchange_kernel, z), name='exchange', ou...]
    all_to_all x3 -> x0, waiting for transfers between devices: 57.1 us -> none  [the longest x1 20.8 us: shards(): lax.all_to_all(field, 'lon', split_axis=2, concat_axis=1, tiled=True)]
    unnamed x123 -> x22, local copies, waits for them, and re-layouts: 35.8 us -> 2.36 us
    convert_element_type x5 -> x0, local copies, waits for them, and re-layouts: 27 us -> none  [the longest x2 10.8 us: channel_mlp(): tokens = spatial.reshape(-1, channels).astype(jnp.float32)]
    all_to_all x3 -> x0, starting transfers between devices: 24.2 us -> none  [the longest x1 11.9 us: shards(): lax.all_to_all(weighted, 'lat', split_axis=0, concat_axis=1, tiled=True)]
    all_to_all x6 -> x0, local copies, waits for them, and re-layouts: 24 us -> none  [the longest x2 8.86 us: shards(): lax.all_to_all(synthesis, 'lat', split_axis=1, concat_axis=0, tiled=True)]
    dot_general x9 -> x0, matrix products: 20.8 us -> none  [the longest x1 7.24 us: channel_mlp(): result = jnp.dot(hidden, w_out, preferred_element_type=jnp.float32)]
    all_to_all x1 -> x0, blocking collectives: 19.3 us -> none  [shards(): lax.all_to_all(spatial_part, 'lon', split_axis=1, concat_axis=2, tiled=True)]
  transfers between devices with their start and end apart: 5 -> 0, of which waited for: 5 -> 0; matrix products, arithmetic and copies ran while one was open for 11% -> 0% of each run, Pallas kernels for 0% -> 0%
where the time goes in v1:
time: 114 us
  Pallas kernels  110 us (96%)
  local copies, waits for them, and re-layouts  3.09 us (3%)
    pallas_call x1, Pallas kernels, exchange(): pl.pallas_call(functools.partial(exchange_kernel, z), name='exchange', ou...  97.8 us
    pallas_call x1, Pallas kernels, local(): pl.pallas_call(functools.partial(local_kernel, z, rstep), name='local', g...  12.5 us
    unnamed x22, local copies, waits for them, and re-layouts  2.36 us

profile of v1, /device:TPU:1, one launch (start us, length us, event | category | flops | bytes accessed | tf_op | source)
XLA Modules:
  0.0 114.2 jit_solution(15889889562608306318)
XLA Ops:
  0.6 0.7 broadcast_in_dim.16.weight_ref
  1.4 0.0 copy-start
  1.4 0.0 copy-start.2
  1.4 0.0 copy-start.3
  1.4 0.0 copy-start.5
  1.4 0.0 copy-start.6
  1.4 0.0 copy-start.7
  1.4 0.0 copy-start.8
  1.5 0.0 copy-start.9
  1.5 0.0 copy-start.10
  1.5 97.8 %exchange.1 = (bf16[16,96,512]{2,1,0:T(8,128)(2,1)}, f32[64,512]{1,0:T(8,128)}) custom-call(f32[12]{0:T(128)} %quad_ref.1, bf16[12,96,512]{2,1,0:T(8,128)(2,1)} %field_ref.3, bf16[12,384,384]{2,1,0:T(8,128)(2,1)} %leg_ref.1, f32[384,512]{1,0:T(8,128)} %fr_ref.1, f32[384,512]{1,0:T(8,128)} %fi_ref.1, bf16[768,768]{1,0:T(8,128)(2,1)} %constant.10.clone.fwd_ref, ...), custom_call_target="tpu_custom_call" | custom-call | flops 1811939328 | bytes 16777216 | tf_op jit(solution)/shard_map/exchange/pallas_call | solution.py:393
  99.3 0.0 copy-done
  99.3 0.0 copy-done.2
  99.3 0.0 copy-done.3
  99.3 0.0 copy-done.5
  99.3 0.0 copy-done.6
  99.4 0.0 copy-done.7
  99.4 0.0 copy-done.8
  99.4 0.0 copy-done.9
  99.4 0.0 copy-done.10
  99.4 0.0 copy-start.1
  99.4 1.4 %copy-done.1 = bf16[16,96,512]{2,1,0:T(8,128)(2,1)S(1)} copy-done((bf16[16,96,512]{2,1,0:T(8,128)(2,1)S(1)}, bf16[16,96,512]{2,1,0:T(8,128)(2,1)}, u32[]{:S(2)}) %copy-start.1) | copy-done | bytes 1572888
  100.8 0.0 copy-start.4
  100.8 0.9 copy-done.4
  101.7 12.5 %local.1 = (bf16[12,96,512]{2,1,0:T(8,128)(2,1)}, bf16[12,96,512]{2,1,0:T(8,128)(2,1)}) custom-call(s32[12,12]{1,0:T(8,128)S(1)} %copy-done.5, s32[12,12]{1,0:T(8,128)S(1)} %copy-done.6, f32[12,12]{1,0:T(8,128)S(1)} %copy-done.7, s32[1]{0:T(128)} %bitcast.place, bf16[16,96,512]{2,1,0:T(8,128)(2,1)S(1)} %copy-done.1, f32[64,512]{1,0:T(8,128)S(1)} %copy-done.4, ...), custom_call_target="tpu_custom_call" | custom-call | tf_op jit(solution)/shard_map/local/pallas_call | solution.py:528
Async XLA Ops:
  1.4 97.9 %copy-start = (bf16[12,96,512]{2,1,0:T(8,128)(2,1)S(1)}, bf16[12,96,512]{2,1,0:T(8,128)(2,1)}, u32[]{:S(2)}) copy-start(bf16[12,96,512]{2,1,0:T(8,128)(2,1)} %field_ref.3) | copy-start | bytes 3538948
  1.4 97.9 %copy-start.2 = (bf16[512,1024]{1,0:T(8,128)(2,1)S(1)}, bf16[512,1024]{1,0:T(8,128)(2,1)}, u32[]{:S(2)}) copy-start(bf16[512,1024]{1,0:T(8,128)(2,1)} %win_ref.1) | copy-start | bytes 3145732
  1.4 97.9 %copy-start.3 = (bf16[1024,512]{1,0:T(8,128)(2,1)S(1)}, bf16[1024,512]{1,0:T(8,128)(2,1)}, u32[]{:S(2)}) copy-start(bf16[1024,512]{1,0:T(8,128)(2,1)} %wout_ref.1) | copy-start | bytes 3145732
  1.4 97.9 %copy-start.5 = (s32[12,12]{1,0:T(8,128)S(1)}, s32[12,12]{1,0:T(8,128)}, u32[]{:S(2)}) copy-start(s32[12,12]{1,0:T(8,128)} %neighbour.1) | copy-start | bytes 1732
  1.4 97.9 %copy-start.6 = (s32[12,12]{1,0:T(8,128)S(1)}, s32[12,12]{1,0:T(8,128)}, u32[]{:S(2)}) copy-start(s32[12,12]{1,0:T(8,128)} %basis.1) | copy-start | bytes 1732
  1.4 97.9 %copy-start.7 = (f32[12,12]{1,0:T(8,128)S(1)}, f32[12,12]{1,0:T(8,128)}, u32[]{:S(2)}) copy-start(f32[12,12]{1,0:T(8,128)} %quad.1) | copy-start | bytes 1732
  1.4 97.9 %copy-start.8 = (f32[1024]{0:T(1024)S(1)}, f32[1024]{0:T(1024)}, u32[]{:S(2)}) copy-start(f32[1024]{0:T(1024)} %param.27) | copy-start | bytes 12292
  1.5 97.9 %copy-start.9 = (f32[512]{0:T(512)S(1)}, f32[512]{0:T(512)}, u32[]{:S(2)}) copy-start(f32[512]{0:T(512)} %param.25) | copy-start | bytes 6148
  1.5 97.9 %copy-start.10 = (f32[512]{0:T(512)S(1)}, f32[512]{0:T(512)}, u32[]{:S(2)}) copy-start(f32[512]{0:T(512)} %param.29) | copy-start | bytes 6148
  99.4 1.4 %copy-start.1 = (bf16[16,96,512]{2,1,0:T(8,128)(2,1)S(1)}, bf16[16,96,512]{2,1,0:T(8,128)(2,1)}, u32[]{:S(2)}) copy-start(bf16[16,96,512]{2,1,0:T(8,128)(2,1)} %get-tuple-element.4.wave_ref) | copy-start | bytes 4718596
  100.8 0.9 copy-start.4

commit v2 on v1

--- a/solution.py
+++ b/solution.py
@@ -53,6 +53,10 @@
         self.chunks = self.trow // self.step
         self.mr = 2 * self.wper
         self.blk = self.step * self.mr
+        self.deep = max(self.groups // 8, 1)
+
+    def turn(self, c, half):
+        return c + half * (self.chunks - 1 - 2 * c)
 
 
 def exchange_kernel(
@@ -123,29 +127,33 @@
     for k in (0, 2, 3, 4):
         loads[k].start()
 
-    def group_peer(o):
-        nz = max(G // 8, 1)
-        a = (o % nz) * 3 % nz
-        b = o // nz
-        per = G // nz
-        here = me // (per // 2) % nz if nz > 1 else 0
-        half = me // (G // 2)
-        low = me % (per // 2)
-        zz = (here + a) % nz
-        other = (half * (per // 2) + low + b) % per
-        peer = (other // (per // 2)) * (G // 2) + zz * (per // 2) + other % (per // 2)
-        return peer
-
-    def group_id(peer):
-        return {"lat": peer // z.nh, "lon": (peer % z.nh) * z.nq + q}
+    low = G // z.deep // 2
+    deep = lax.rem(lax.div(me, low), z.deep)
+    flat = lax.div(me, G // 2) * low + lax.rem(me, low)
+    levels = [lax.rem(deep + 3 * a % z.deep, z.deep) for a in range(z.deep)]
+
+    def each_peer(act):
+        def shift(b, skip):
+            other = lax.rem(flat + b, 2 * low)
+            half = lax.div(other, low)
+            side = lax.rem(other, low)
+            column = lax.rem(side, z.nh) * z.nq + q
+            first = half * (G // 2) + side
+            row = half * (z.ni // 2) + lax.div(side, z.nh)
+            for a in range(skip, z.deep):
+                act(
+                    first + levels[a] * low,
+                    {"lat": row + levels[a] * (low // z.nh), "lon": column},
+                )
+
+        def body(b, carry):
+            shift(b, 0)
+            return carry
+
+        shift(0, 1)
+        lax.fori_loop(1, 2 * low, body, 0)
 
     barrier = pltpu.get_barrier_semaphore()
-
-    def greet(o, carry):
-        pl.semaphore_signal(
-            barrier, inc=1, device_id=group_id(group_peer(o)), device_id_type=MESH
-        )
-        return carry
 
     def greet_lon(o, carry):
         hh = (h + o // (z.nq - 1)) % z.nh
@@ -157,8 +165,13 @@
 
     lon_only = z.nh * (z.nq - 1)
     lax.fori_loop(0, lon_only, greet_lon, 0)
-    lax.fori_loop(1, G, greet, 0)
-    pl.semaphore_wait(barrier, lon_only + G - 1)
+    each_peer(
+        lambda peer, to: pl.semaphore_signal(
+            barrier, inc=1, device_id=to, device_id_type=MESH
+        )
+    )
+    with jax.named_scope("barrier"):
+        pl.semaphore_wait(barrier, lon_only + G - 1)
 
     for c in range(z.chunks):
 
@@ -182,11 +195,13 @@
             ).start()
             return carry
 
-        lax.fori_loop(1, z.nj, send_a, 0)
+        with jax.named_scope("a_start"):
+            lax.fori_loop(1, z.nj, send_a, 0)
 
     loads[0].wait()
-    for w in range(z.wper):
-        ltrans[w] = ltab[w].T
+    with jax.named_scope("trans"):
+        for w in range(z.wper):
+            ltrans[w] = ltab[w].T
     loads[1].wait()
     own.wait()
 
@@ -198,33 +213,35 @@
             send[c, s] = load_block(s).astype(BF16)
             return carry
 
-        lax.fori_loop(0, G, pack, 0, unroll=8)
+        with jax.named_scope("pack"):
+            lax.fori_loop(0, G, pack, 0, unroll=8)
         recv[c, me] = send[c, me]
 
-        def start(o, carry):
-            peer = group_peer(o)
+        def start(peer, to):
             pltpu.make_async_remote_copy(
                 src_ref=send.at[c, peer],
                 dst_ref=recv.at[c, me],
                 send_sem=send_sem,
                 recv_sem=recv_sem.at[c],
-                device_id=group_id(peer),
+                device_id=to,
                 device_id_type=MESH,
             ).start()
-            return carry
-
-        lax.fori_loop(1, G, start, 0)
+
+        with jax.named_scope("bc_start"):
+            each_peer(start)
 
     for c in range(z.chunks):
         span = z.cols * (z.nj - 1)
-        await_bytes(cols_in.at[pl.ds(c * z.step, z.step), pl.ds(0, span), :], a_recv.at[c])
-        rhs = jnp.concatenate([cols_in[c * z.step + k] for k in range(z.step)], axis=1)
-        spec = jnp.dot(fwd[...], rhs, preferred_element_type=F32)
-        for k in range(z.step):
-            quad = quad_ref[h * z.trow + c * z.step + k]
-            part = spec[:, k * LANES : (k + 1) * LANES] * quad
-            for p in range(z.mr):
-                stage[pl.ds(k * z.mr + p, G, stride=z.blk), :] = part[p * G : (p + 1) * G]
+        with jax.named_scope("a_wait"):
+            await_bytes(cols_in.at[pl.ds(c * z.step, z.step), pl.ds(0, span), :], a_recv.at[c])
+        with jax.named_scope("dft"):
+            rhs = jnp.concatenate([cols_in[c * z.step + k] for k in range(z.step)], axis=1)
+            spec = jnp.dot(fwd[...], rhs, preferred_element_type=F32)
+            for k in range(z.step):
+                quad = quad_ref[h * z.trow + c * z.step + k]
+                part = spec[:, k * LANES : (k + 1) * LANES] * quad
+                for p in range(z.mr):
+                    stage[pl.ds(k * z.mr + p, G, stride=z.blk), :] = part[p * G : (p + 1) * G]
         pack_and_send(
             c,
             send1,
@@ -235,7 +252,8 @@
         )
 
     for c in range(z.chunks):
-        await_bytes(recv1.at[c, pl.ds(0, G - 1)], b_recv.at[c])
+        with jax.named_scope("b_wait"):
+            await_bytes(recv1.at[c, pl.ds(0, G - 1)], b_recv.at[c])
 
         def unpack(s, carry):
             at = pl.multiple_of(s * (z.blk * z.chunks) + c * z.blk, 8)
@@ -247,19 +265,20 @@
     for k in (2, 3, 4):
         loads[k].wait()
 
-    for w in range(z.wper):
-        weighted = jnp.concatenate(
-            [wide[pl.ds(2 * w + r, z.nlat, stride=z.mr), :] for r in range(2)], axis=1
-        ).astype(BF16)
-        coef = jnp.dot(ltab[w], weighted, preferred_element_type=F32)
-        re = coef[:, :LANES]
-        im = coef[:, LANES:]
-        a = gr[...]
-        b = gi[...]
-        filt = jnp.concatenate([a * re - b * im, a * im + b * re], axis=1).astype(BF16)
-        syn = jnp.dot(ltrans[w], filt, preferred_element_type=F32)
-        for r in range(2):
-            wide[pl.ds(2 * w + r, z.nlat, stride=z.mr), :] = syn[:, r * LANES : (r + 1) * LANES]
+    with jax.named_scope("legendre"):
+        for w in range(z.wper):
+            weighted = jnp.concatenate(
+                [wide[pl.ds(2 * w + r, z.nlat, stride=z.mr), :] for r in range(2)], axis=1
+            ).astype(BF16)
+            coef = jnp.dot(ltab[w], weighted, preferred_element_type=F32)
+            re = coef[:, :LANES]
+            im = coef[:, LANES:]
+            a = gr[...]
+            b = gi[...]
+            filt = jnp.concatenate([a * re - b * im, a * im + b * re], axis=1).astype(BF16)
+            syn = jnp.dot(ltrans[w], filt, preferred_element_type=F32)
+            for r in range(2):
+                wide[pl.ds(2 * w + r, z.nlat, stride=z.mr), :] = syn[:, r * LANES : (r + 1) * LANES]
 
     for c in range(z.chunks):
         pack_and_send(
@@ -269,41 +288,58 @@
             c_send,
             c_recv,
             lambda s: wide[
-                pl.ds(pl.multiple_of(s * (z.blk * z.chunks) + c * z.blk, 8), z.blk), :
+                pl.ds(
+                    pl.multiple_of(
+                        s * (z.blk * z.chunks) + z.turn(c, lax.rem(s, z.nh)) * z.blk, 8
+                    ),
+                    z.blk,
+                ),
+                :,
             ],
         )
 
     own_copies = []
+    moves = []
+
+    def await_rows(c):
+        span = z.cols * (z.nj - 1)
+        own_copies[2 * c].wait()
+        own_copies[2 * c + 1].wait()
+        await_bytes(wbuf.at[pl.ds(c * z.step, z.step), pl.ds(0, span), :], d_recv.at[c])
+        await_bytes(ebuf.at[c, pl.ds(0, z.nj - 1)], e_recv.at[c])
+
     for c in range(z.chunks):
-        await_bytes(recv2.at[c, pl.ds(0, G - 1)], c_recv.at[c])
+        with jax.named_scope("c_wait"):
+            await_bytes(recv2.at[c, pl.ds(0, G - 1)], c_recv.at[c])
 
         def unpack(s, carry):
             stage[pl.ds(pl.multiple_of(s * z.blk, 8), z.blk), :] = recv2[c, s].astype(F32)
             return carry
 
-        lax.fori_loop(0, G, unpack, 0, unroll=8)
-        modes = jnp.concatenate(
-            [
-                jnp.concatenate(
-                    [stage[pl.ds(k * z.mr + p, G, stride=z.blk), :] for p in range(z.mr)],
-                    axis=0,
-                )
-                for k in range(z.step)
-            ],
-            axis=1,
-        ).astype(BF16)
-        full = jnp.dot(inv[...], modes, preferred_element_type=F32)
-        edge_rows = 4 * z.step
-        for k in range(z.step):
-            half = full[:, k * LANES : (k + 1) * LANES]
-            wbuf[c * z.step + k] = half[: z.nlon].astype(BF16)
-            for e in range(4):
-                at = z.nlon + e * z.nj
-                ebuf32[pl.ds(k * 4 + e, z.nj, stride=edge_rows), :] = half[at : at + z.nj]
-        for p in range(z.nj):
-            ebuf[c, p] = ebuf32[p * edge_rows : (p + 1) * edge_rows, :].astype(BF16).astype(F32)
-
-        row = HALO + h * z.trow + c * z.step
+        with jax.named_scope("idft"):
+            lax.fori_loop(0, G, unpack, 0, unroll=8)
+            modes = jnp.concatenate(
+                [
+                    jnp.concatenate(
+                        [stage[pl.ds(k * z.mr + p, G, stride=z.blk), :] for p in range(z.mr)],
+                        axis=0,
+                    )
+                    for k in range(z.step)
+                ],
+                axis=1,
+            ).astype(BF16)
+            full = jnp.dot(inv[...], modes, preferred_element_type=F32)
+            edge_rows = 4 * z.step
+            for k in range(z.step):
+                half = full[:, k * LANES : (k + 1) * LANES]
+                wbuf[c * z.step + k] = half[: z.nlon].astype(BF16)
+                for e in range(4):
+                    at = z.nlon + e * z.nj
+                    ebuf32[pl.ds(k * 4 + e, z.nj, stride=edge_rows), :] = half[at : at + z.nj]
+            for p in range(z.nj):
+                ebuf[c, p] = ebuf32[p * edge_rows : (p + 1) * edge_rows, :].astype(BF16).astype(F32)
+
+        row = HALO + h * z.trow + z.turn(c, h) * z.step
 
         def wave_pair(p):
             return (
@@ -337,52 +373,55 @@
                 ).start()
             return carry
 
-        lax.fori_loop(1, z.nj, send_d, 0)
+        with jax.named_scope("d_start"):
+            lax.fori_loop(1, z.nj, send_d, 0)
         for n, (src, dst) in enumerate((wave_pair(j), edge_pair(j))):
             copy = pltpu.make_async_copy(src, dst, out_own.at[c, n])
             copy.start()
             own_copies.append(copy)
 
-    for copy in own_copies:
-        copy.wait()
-    for c in range(z.chunks):
-        span = z.cols * (z.nj - 1)
-        await_bytes(wbuf.at[pl.ds(c * z.step, z.step), pl.ds(0, span), :], d_recv.at[c])
-        await_bytes(ebuf.at[c, pl.ds(0, z.nj - 1)], e_recv.at[c])
-
-    last = z.rows + HALO
-    moves = []
-    for n, (src_row, dst_row, to) in enumerate(
-        ((HALO, last, (i + z.ni - 1) % z.ni), (last - HALO, 0, (i + 1) % z.ni))
-    ):
-        for f, (src, dst) in enumerate(
-            (
-                (wave_out.at[pl.ds(src_row, HALO)], wave_out.at[pl.ds(dst_row, HALO)]),
+        if c != 1:
+            continue
+        with jax.named_scope("h_start"):
+            await_rows(0)
+        last = z.rows + HALO
+        for n, (src_row, dst_row, to) in enumerate(
+            ((HALO, last, (i + z.ni - 1) % z.ni), (last - HALO, 0, (i + 1) % z.ni))
+        ):
+            for f, (src, dst) in enumerate(
                 (
-                    edge_out.at[pl.ds(src_row * 4, HALO * 4)],
-                    edge_out.at[pl.ds(dst_row * 4, HALO * 4)],
-                ),
-            )
-        ):
-            move = pltpu.make_async_remote_copy(
-                src_ref=src,
-                dst_ref=dst,
-                send_sem=h_send.at[n, f],
-                recv_sem=h_recv.at[n, f],
-                device_id={"lat": to, "lon": j},
-                device_id_type=MESH,
-            )
-            move.start()
-            moves.append(move)
-    for move in moves:
-        move.wait()
+                    (wave_out.at[pl.ds(src_row, HALO)], wave_out.at[pl.ds(dst_row, HALO)]),
+                    (
+                        edge_out.at[pl.ds(src_row * 4, HALO * 4)],
+                        edge_out.at[pl.ds(dst_row * 4, HALO * 4)],
+                    ),
+                )
+            ):
+                move = pltpu.make_async_remote_copy(
+                    src_ref=src,
+                    dst_ref=dst,
+                    send_sem=h_send.at[n, f],
+                    recv_sem=h_recv.at[n, f],
+                    device_id={"lat": to, "lon": j},
+                    device_id_type=MESH,
+                )
+                move.start()
+                moves.append(move)
+
+    with jax.named_scope("d_wait"):
+        for c in range(1, z.chunks):
+            await_rows(c)
+    with jax.named_scope("h_wait"):
+        for move in moves:
+            move.wait()
 
     span = z.cols * (z.nj - 1)
-    await_bytes(wbuf.at[:, pl.ds(0, span), :], a_send)
-    await_bytes(send1.at[:, pl.ds(0, G - 1)], b_send)
-    await_bytes(send2.at[:, pl.ds(0, G - 1)], c_send)
-    await_bytes(wbuf.at[:, pl.ds(0, span), :], d_send)
-    await_bytes(ebuf.at[:, pl.ds(0, z.nj - 1)], e_send)
+    with jax.named_scope("drain"):
+        await_bytes(wbuf.at[:, pl.ds(0, span), :], a_send)
+        await_bytes(send1.at[:, pl.ds(0, G - 1)], b_send)
+        await_bytes(send2.at[:, pl.ds(0, G - 1)], c_send)
+        await_bytes(wbuf.at[:, pl.ds(0, span), :], d_send)
+        await_bytes(ebuf.at[:, pl.ds(0, z.nj - 1)], e_send)
 
 
 def exchange(z, field, quad, legendre, fr, fi, fwd, inv):

time: 114 us -> 107 us (0.939)
  Pallas kernels: 110 us -> 103 us
    pallas_call x1, Pallas kernels: 97.8 us -> 90.2 us  [exchange(): pl.pallas_call(functools.partial(exchange_kernel, z), name='exchange', ou...]
where the time goes in v2:
time: 107 us
  Pallas kernels  103 us (96%)
  local copies, waits for them, and re-layouts  3.09 us (3%)
    pallas_call x1, Pallas kernels, exchange(): pl.pallas_call(functools.partial(exchange_kernel, z), name='exchange', ou...  90.2 us
    pallas_call x1, Pallas kernels, local(): pl.pallas_call(functools.partial(local_kernel, z, rstep), name='local', g...  12.5 us
    unnamed x22, local copies, waits for them, and re-layouts  2.36 us

profile of v2, /device:TPU:1, one launch (start us, length us, event | category | flops | bytes accessed | tf_op | source)
XLA Modules:
  0.0 106.6 jit_solution(12519081380631474701)
XLA Ops:
  0.6 0.7 broadcast_in_dim.16.weight_ref
  1.4 0.0 copy-start
  1.4 0.0 copy-start.2
  1.4 0.0 copy-start.3
  1.4 0.0 copy-start.5
  1.4 0.0 copy-start.6
  1.4 0.0 copy-start.7
  1.4 0.0 copy-start.8
  1.5 0.0 copy-start.9
  1.5 0.0 copy-start.10
  1.5 90.2 %exchange.1 = (bf16[16,96,512]{2,1,0:T(8,128)(2,1)}, f32[64,512]{1,0:T(8,128)}) custom-call(f32[12]{0:T(128)} %quad_ref.1, bf16[12,96,512]{2,1,0:T(8,128)(2,1)} %field_ref.3, bf16[12,384,384]{2,1,0:T(8,128)(2,1)} %leg_ref.1, f32[384,512]{1,0:T(8,128)} %fr_ref.1, f32[384,512]{1,0:T(8,128)} %fi_ref.1, bf16[768,768]{1,0:T(8,128)(2,1)} %constant.10.clone.fwd_ref, ...), custom_call_target="tpu_custom_call" | custom-call | flops 1811939328 | bytes 16777216 | tf_op jit(solution)/shard_map/exchange/pallas_call | solution.py:432
  91.7 0.0 copy-done
  91.7 0.0 copy-done.2
  91.7 0.0 copy-done.3
  91.7 0.0 copy-done.5
  91.8 0.0 copy-done.6
  91.8 0.0 copy-done.7
  91.8 0.0 copy-done.8
  91.8 0.0 copy-done.9
  91.8 0.0 copy-done.10
  91.8 0.0 copy-start.1
  91.8 1.4 %copy-done.1 = bf16[16,96,512]{2,1,0:T(8,128)(2,1)S(1)} copy-done((bf16[16,96,512]{2,1,0:T(8,128)(2,1)S(1)}, bf16[16,96,512]{2,1,0:T(8,128)(2,1)}, u32[]{:S(2)}) %copy-start.1) | copy-done | bytes 1572888
  93.2 0.0 copy-start.4
  93.2 0.9 copy-done.4
  94.1 12.5 %local.1 = (bf16[12,96,512]{2,1,0:T(8,128)(2,1)}, bf16[12,96,512]{2,1,0:T(8,128)(2,1)}) custom-call(s32[12,12]{1,0:T(8,128)S(1)} %copy-done.5, s32[12,12]{1,0:T(8,128)S(1)} %copy-done.6, f32[12,12]{1,0:T(8,128)S(1)} %copy-done.7, s32[1]{0:T(128)} %bitcast.place, bf16[16,96,512]{2,1,0:T(8,128)(2,1)S(1)} %copy-done.1, f32[64,512]{1,0:T(8,128)S(1)} %copy-done.4, ...), custom_call_target="tpu_custom_call" | custom-call | tf_op jit(solution)/shard_map/local/pallas_call | solution.py:567
Async XLA Ops:
  1.4 90.4 %copy-start = (bf16[12,96,512]{2,1,0:T(8,128)(2,1)S(1)}, bf16[12,96,512]{2,1,0:T(8,128)(2,1)}, u32[]{:S(2)}) copy-start(bf16[12,96,512]{2,1,0:T(8,128)(2,1)} %field_ref.3) | copy-start | bytes 3538948
  1.4 90.4 %copy-start.2 = (bf16[512,1024]{1,0:T(8,128)(2,1)S(1)}, bf16[512,1024]{1,0:T(8,128)(2,1)}, u32[]{:S(2)}) copy-start(bf16[512,1024]{1,0:T(8,128)(2,1)} %win_ref.1) | copy-start | bytes 3145732
  1.4 90.3 %copy-start.3 = (bf16[1024,512]{1,0:T(8,128)(2,1)S(1)}, bf16[1024,512]{1,0:T(8,128)(2,1)}, u32[]{:S(2)}) copy-start(bf16[1024,512]{1,0:T(8,128)(2,1)} %wout_ref.1) | copy-start | bytes 3145732
  1.4 90.3 %copy-start.5 = (s32[12,12]{1,0:T(8,128)S(1)}, s32[12,12]{1,0:T(8,128)}, u32[]{:S(2)}) copy-start(s32[12,12]{1,0:T(8,128)} %neighbour.1) | copy-start | bytes 1732
  1.4 90.3 %copy-start.6 = (s32[12,12]{1,0:T(8,128)S(1)}, s32[12,12]{1,0:T(8,128)}, u32[]{:S(2)}) copy-start(s32[12,12]{1,0:T(8,128)} %basis.1) | copy-start | bytes 1732
  1.4 90.3 %copy-start.7 = (f32[12,12]{1,0:T(8,128)S(1)}, f32[12,12]{1,0:T(8,128)}, u32[]{:S(2)}) copy-start(f32[12,12]{1,0:T(8,128)} %quad.1) | copy-start | bytes 1732
  1.4 90.3 %copy-start.8 = (f32[1024]{0:T(1024)S(1)}, f32[1024]{0:T(1024)}, u32[]{:S(2)}) copy-start(f32[1024]{0:T(1024)} %param.27) | copy-start | bytes 12292
  1.5 90.3 %copy-start.9 = (f32[512]{0:T(512)S(1)}, f32[512]{0:T(512)}, u32[]{:S(2)}) copy-start(f32[512]{0:T(512)} %param.25) | copy-start | bytes 6148
  1.5 90.3 %copy-start.10 = (f32[512]{0:T(512)S(1)}, f32[512]{0:T(512)}, u32[]{:S(2)}) copy-start(f32[512]{0:T(512)} %param.29) | copy-start | bytes 6148
  91.8 1.4 %copy-start.1 = (bf16[16,96,512]{2,1,0:T(8,128)(2,1)S(1)}, bf16[16,96,512]{2,1,0:T(8,128)(2,1)}, u32[]{:S(2)}) copy-start(bf16[16,96,512]{2,1,0:T(8,128)(2,1)} %get-tuple-element.4.wave_ref) | copy-start | bytes 4718596
  93.2 0.9 copy-start.4

commit v3 on v2

v3 whole, which is shorter than its diff:
```python
import functools
import math

import jax
import jax.numpy as jnp
import ml_dtypes
import numpy as np
from jax import lax
from jax.experimental import pallas as pl
from jax.experimental.pallas import tpu as pltpu
from jax.sharding import PartitionSpec as P

HALO = 2
LANES = 128
MESH = pl.DeviceIdType.MESH
BF16 = jnp.bfloat16
F32 = jnp.float32


def tables(nlon, mmax, groups, blocks):
    per = mmax // groups
    waves = np.stack([np.arange(groups) * per + p for p in range(per)])
    waves = np.repeat(waves[:, None, :], 2, axis=1).reshape(-1)
    part = np.broadcast_to(np.array([0, 1])[None, :, None], (per, 2, groups)).reshape(-1)
    cols = nlon // blocks
    edge = np.array([-2, -1, cols, cols + 1])
    halo = (edge[:, None] + np.arange(blocks)[None, :] * cols).reshape(-1) % nlon
    points = np.concatenate([np.arange(nlon), halo])
    angle = (waves[:, None] * points[None, :] % nlon) * (2.0 * math.pi / nlon)
    wave = np.where(part[:, None] == 0, np.cos(angle), -np.sin(angle)) / math.sqrt(nlon)
    factor = np.where(waves == 0, 1.0, 2.0)
    forward = wave[:, :nlon].astype(ml_dtypes.bfloat16)
    inverse = (wave * factor[:, None]).T.astype(ml_dtypes.bfloat16)
    return forward, np.ascontiguousarray(inverse)


class Sizes:
    def __init__(self, mesh, lat_rows, lon_cols, channels, wave_block, degrees):
        self.ni = mesh.shape["lat"]
        self.nj = mesh.shape["lon"]
        self.nq = channels // LANES
        self.nh = self.nj // self.nq
        self.groups = self.ni * self.nh
        self.rows = lat_rows
        self.trow = lat_rows // self.nh
        self.cols = lon_cols
        self.nlon = lon_cols * self.nj
        self.chan = channels
        self.wper = wave_block // self.nh
        self.deg = degrees
        self.nlat = lat_rows * self.ni
        self.step = 2
        self.chunks = self.trow // self.step
        self.mr = 2 * self.wper
        self.blk = self.step * self.mr
        self.deep = max(self.groups // 8, 1)
        self.late = self.mr // 3
        self.early = self.mr - self.late

    def turn(self, c, half):
        return c + half * (self.chunks - 1 - 2 * c)


def block_kernel(
    z,
    quad_hbm,
    neighbour_hbm,
    basis_hbm,
    disco_hbm,
    field_ref,
    leg_ref,
    fr_ref,
    fi_ref,
    fwd_ref,
    inv_ref,
    weight_ref,
    gain_ref,
    win_ref,
    bin_ref,
    wout_ref,
    bout_ref,
    block_out,
    spatial_out,
    quad_ref,
    neighbour,
    basis,
    disco,
    fbuf,
    cols_in,
    ltab,
    ltrans,
    fwd,
    inv,
    gr,
    gi,
    weight,
    gain,
    w_in,
    b_in,
    w_out,
    b_out,
    wrow,
    stage,
    stage_late,
    wide,
    wide_late,
    send1,
    recv1,
    send1_late,
    recv1_late,
    send2,
    recv2,
    wbuf,
    ebuf32,
    ebuf,
    vbuf,
    hbuf,
    padded,
    load_sem,
    a_send,
    a_recv,
    b_send,
    b_recv,
    c_send,
    c_recv,
    d_send,
    d_recv,
    e_send,
    e_recv,
    h_send,
    h_recv,
):
    i = lax.axis_index("lat")
    j = lax.axis_index("lon")
    h = j // z.nq
    q = j % z.nq
    me = i * z.nh + h
    lane0 = pl.multiple_of(q * LANES, LANES)
    G = z.groups
    early, late, step = z.early, z.late, z.step
    here = pl.ds(pl.multiple_of(j * z.cols, 16), z.cols)

    def load(n, src, dst):
        copy = pltpu.make_async_copy(src, dst, load_sem.at[n])
        copy.start()
        return copy

    field_load = load(0, field_ref, fbuf)
    leg_load = load(1, leg_ref.at[pl.ds(h * z.wper, z.wper)], ltab)
    fwd_load = load(2, fwd_ref, fwd)

    low = G // z.deep // 2
    deep = lax.rem(lax.div(me, low), z.deep)
    flat = lax.div(me, G // 2) * low + lax.rem(me, low)
    levels = [lax.rem(deep + 3 * a % z.deep, z.deep) for a in range(z.deep)]

    def each_peer(act):
        def shift(b, skip):
            other = lax.rem(flat + b, 2 * low)
            half = lax.div(other, low)
            side = lax.rem(other, low)
            column = lax.rem(side, z.nh) * z.nq + q
            first = half * (G // 2) + side
            row = half * (z.ni // 2) + lax.div(side, z.nh)
            for a in range(skip, z.deep):
                act(
                    first + levels[a] * low,
                    {"lat": row + levels[a] * (low // z.nh), "lon": column},
                )

        def body(b, carry):
            shift(b, 0)
            return carry

        shift(0, 1)
        lax.fori_loop(1, 2 * low, body, 0)

    barrier = pltpu.get_barrier_semaphore()

    def greet_lon(o, carry):
        hh = (h + o // (z.nq - 1)) % z.nh
        qq = (q + 1 + o % (z.nq - 1)) % z.nq
        pl.semaphore_signal(
            barrier, inc=1, device_id={"lat": i, "lon": hh * z.nq + qq}, device_id_type=MESH
        )
        return carry

    lon_only = z.nh * (z.nq - 1)
    with jax.named_scope("greet"):
        lax.fori_loop(0, lon_only, greet_lon, 0)
        each_peer(
            lambda peer, to: pl.semaphore_signal(
                barrier, inc=1, device_id=to, device_id_type=MESH
            )
        )
    rest = [
        load(n + 3, src, dst)
        for n, (src, dst) in enumerate(
            (
                (inv_ref, inv),
                (fr_ref.at[:, pl.ds(lane0, LANES)], gr),
                (fi_ref.at[:, pl.ds(lane0, LANES)], gi),
                (weight_ref, weight),
                (gain_ref, gain),
                (win_ref, w_in),
                (bin_ref, b_in),
                (wout_ref, w_out),
                (bout_ref, b_out),
                (quad_hbm, quad_ref),
                (neighbour_hbm, neighbour),
                (basis_hbm, basis),
                (disco_hbm, disco),
            )
        )
    ]
    field_load.wait()
    cols_in[:, here, :] = fbuf[pl.ds(h * z.trow, z.trow), :, pl.ds(lane0, LANES)]
    with jax.named_scope("barrier"):
        pl.semaphore_wait(barrier, lon_only + G - 1)

    def start_a(c):
        def send_a(o, carry):
            p = lax.rem(j + o, z.nj)
            hp = lax.div(p, z.nq)
            qp = lax.rem(p, z.nq)
            pltpu.make_async_remote_copy(
                src_ref=fbuf.at[
                    pl.ds(hp * z.trow + c * step, step),
                    :,
                    pl.ds(pl.multiple_of(qp * LANES, LANES), LANES),
                ],
                dst_ref=cols_in.at[pl.ds(c * step, step), here, :],
                send_sem=a_send,
                recv_sem=a_recv.at[c],
                device_id={"lat": i, "lon": p},
                device_id_type=MESH,
            ).start()
            return carry

        lax.fori_loop(1, z.nj, send_a, 0)

    def await_bytes(ref, sem):
        pltpu.make_async_copy(ref, ref, sem).wait()

    others = pl.ds(0, z.cols * (z.nj - 1))

    for c in range(z.chunks):
        start_a(c)
    leg_load.wait()
    with jax.named_scope("trans"):
        for w in range(z.wper):
            ltrans[w] = ltab[w].T
    rest[3].wait()
    rest[9].wait()
    for r in range(weight.shape[0]):
        wrow[r] = weight[r : r + 1, :]
    fwd_load.wait()

    def each_group(act):
        def body(s, carry):
            act(s)
            return carry

        lax.fori_loop(0, G, body, 0, unroll=8)

    def spread(src, dst, send_sem, recv_sem):
        def start(peer, to):
            pltpu.make_async_remote_copy(
                src_ref=src(peer),
                dst_ref=dst,
                send_sem=send_sem,
                recv_sem=recv_sem,
                device_id=to,
                device_id_type=MESH,
            ).start()

        with jax.named_scope("start"):
            each_peer(start)

    def rows_of(s, size):
        return pl.ds(pl.multiple_of(s * size, 8), size)

    for c in range(z.chunks):
        with jax.named_scope("a_wait"):
            await_bytes(cols_in.at[pl.ds(c * step, step), others, :], a_recv.at[c])
        with jax.named_scope("dft"):
            rhs = jnp.concatenate([cols_in[c * step + k] for k in range(step)], axis=1)
            spec = jnp.dot(fwd[...], rhs, preferred_element_type=F32)
            for k in range(step):
                quad = quad_ref[h * z.trow + c * step + k]
                part = spec[:, k * LANES : (k + 1) * LANES] * quad
                for p in range(z.mr):
                    piece = part[p * G : (p + 1) * G]
                    if p < early:
                        stage[pl.ds(k * early + p, G, stride=step * early), :] = piece
                    else:
                        at = (c * step + k) * late + p - early
                        stage_late[pl.ds(at, G, stride=z.trow * late), :] = piece

        def pack(s):
            send1[c, s] = stage[rows_of(s, step * early), :].astype(BF16)

        each_group(pack)
        recv1[c, me] = send1[c, me]
        spread(lambda peer: send1.at[c, peer], recv1.at[c, me], b_send.at[0], b_recv.at[c])

    def pack(s):
        send1_late[s] = stage_late[rows_of(s, z.trow * late), :].astype(BF16)

    each_group(pack)
    recv1_late[me] = send1_late[me]
    spread(
        lambda peer: send1_late.at[peer],
        recv1_late.at[me],
        b_send.at[1],
        b_recv.at[z.chunks],
    )

    for copy in rest[1:3]:
        copy.wait()

    def legendre(buf, count, first):
        for w in range(count // 2):
            weighted = jnp.concatenate(
                [buf[pl.ds(2 * w + r, z.nlat, stride=count), :] for r in range(2)], axis=1
            ).astype(BF16)
            coef = jnp.dot(ltab[first + w], weighted, preferred_element_type=F32)
            re = coef[:, :LANES]
            im = coef[:, LANES:]
            a = gr[...]
            b = gi[...]
            filt = jnp.concatenate([a * re - b * im, a * im + b * re], axis=1).astype(BF16)
            syn = jnp.dot(ltrans[first + w], filt, preferred_element_type=F32)
            for r in range(2):
                buf[pl.ds(2 * w + r, z.nlat, stride=count), :] = syn[
                    :, r * LANES : (r + 1) * LANES
                ]

    def pack_back(buf, count, c, at):
        def pack(s):
            first = (s * z.chunks + z.turn(c, lax.rem(s, z.nh))) * (step * count)
            rows = pl.ds(pl.multiple_of(first, 8), step * count)
            send2[c, s, at : at + step * count, :] = buf[rows, :].astype(BF16)

        each_group(pack)

    def spread_back(c):
        spread(lambda peer: send2.at[c, peer], recv2.at[c, me], c_send, c_recv.at[c])

    top = pl.ds(0, step * early)
    bottom = pl.ds(step * early, step * late)

    for c in range(z.chunks):
        with jax.named_scope("b_wait"):
            await_bytes(recv1.at[c, pl.ds(0, G - 1)], b_recv.at[c])

        def unpack(s):
            first = s * (z.trow * early) + c * step * early
            wide[pl.ds(pl.multiple_of(first, 8), step * early), :] = recv1[c, s].astype(F32)

        each_group(unpack)
    with jax.named_scope("legendre"):
        legendre(wide, early, 0)
    pack_back(wide, early, 0, 0)
    spread(
        lambda peer: send2.at[0, peer, top], recv2.at[0, me, top], c_send, c_recv.at[0]
    )
    for c in range(1, z.chunks):
        pack_back(wide, early, c, 0)
    with jax.named_scope("b_wait"):
        await_bytes(recv1_late.at[pl.ds(0, G - 1)], b_recv.at[z.chunks])

    def unpack(s):
        wide_late[rows_of(s, z.trow * late), :] = recv1_late[s].astype(F32)

    each_group(unpack)
    with jax.named_scope("legendre"):
        legendre(wide_late, late, early // 2)
    for c in range(z.chunks):
        pack_back(wide_late, late, c, step * early)
        if c == 0:
            spread(
                lambda peer: send2.at[0, peer, bottom],
                recv2.at[0, me, bottom],
                c_send,
                c_recv.at[0],
            )
        elif c == 1:
            spread_back(c)
        recv2[c, me] = send2[c, me]

    edge_rows = 4 * step
    span = z.rows + 2 * HALO
    moves = []
    for copy in rest[:1] + rest[4:9] + rest[10:]:
        copy.wait()

    def await_rows(c):
        await_bytes(wbuf.at[pl.ds(c * step, step), others, :], d_recv.at[c])
        await_bytes(ebuf.at[c, pl.ds(0, z.nj - 1)], e_recv.at[c])

    for c in range(z.chunks):
        with jax.named_scope("c_wait"):
            await_bytes(recv2.at[c, pl.ds(0, G - 1)], c_recv.at[c])

        def unpack(s):
            stage[rows_of(s, z.blk), :] = recv2[c, s].astype(F32)

        each_group(unpack)
        with jax.named_scope("idft"):
            modes = []
            for k in range(step):
                starts = [k * early + p for p in range(early)]
                starts += [step * early + k * late + p for p in range(late)]
                modes.append(
                    jnp.concatenate(
                        [stage[pl.ds(at, G, stride=z.blk), :] for at in starts], axis=0
                    )
                )
            full = jnp.dot(
                inv[...],
                jnp.concatenate(modes, axis=1).astype(BF16),
                preferred_element_type=F32,
            )
            for k in range(step):
                half = full[:, k * LANES : (k + 1) * LANES]
                wbuf[c * step + k] = half[: z.nlon].astype(BF16)
                for e in range(4):
                    at = z.nlon + e * z.nj
                    ebuf32[pl.ds(k * 4 + e, z.nj, stride=edge_rows), :] = half[at : at + z.nj]
            for p in range(z.nj):
                piece = ebuf32[p * edge_rows : (p + 1) * edge_rows, :]
                ebuf[c, p] = piece.astype(BF16).astype(F32)

        row = HALO + h * z.trow + z.turn(c, h) * step
        edge_at = pl.ds(pl.multiple_of(row * 4, 8), edge_rows)
        lanes = pl.ds(lane0, LANES)

        def send_d(o, carry):
            p = lax.rem(j + o, z.nj)
            there = pl.ds(pl.multiple_of(p * z.cols, 16), z.cols)
            for src, dst, ss, rs in (
                (
                    wbuf.at[pl.ds(c * step, step), there, :],
                    vbuf.at[pl.ds(row, step), :, lanes],
                    d_send,
                    d_recv.at[c],
                ),
                (ebuf.at[c, p], hbuf.at[edge_at, lanes], e_send, e_recv.at[c]),
            ):
                pltpu.make_async_remote_copy(
                    src_ref=src,
                    dst_ref=dst,
                    send_sem=ss,
                    recv_sem=rs,
                    device_id={"lat": i, "lon": p},
                    device_id_type=MESH,
                ).start()
            return carry

        lax.fori_loop(1, z.nj, send_d, 0)
        if c + 2 < z.chunks:
            spread_back(c + 2)
        vbuf[pl.ds(row, step), :, lanes] = wbuf[pl.ds(c * step, step), here, :]
        hbuf[edge_at, lanes] = ebuf[c, j]

        if c != 1:
            continue
        with jax.named_scope("h_start"):
            await_rows(0)
        last = z.rows + HALO
        for n, (src_row, dst_row, to) in enumerate(
            ((HALO, last, (i + z.ni - 1) % z.ni), (last - HALO, 0, (i + 1) % z.ni))
        ):
            for f, (src, dst) in enumerate(
                (
                    (vbuf.at[pl.ds(src_row, HALO)], vbuf.at[pl.ds(dst_row, HALO)]),
                    (
                        hbuf.at[pl.ds(src_row * 4, HALO * 4)],
                        hbuf.at[pl.ds(dst_row * 4, HALO * 4)],
                    ),
                )
            ):
                move = pltpu.make_async_remote_copy(
                    src_ref=src,
                    dst_ref=dst,
                    send_sem=h_send.at[n, f],
                    recv_sem=h_recv.at[n, f],
                    device_id={"lat": to, "lon": j},
                    device_id_type=MESH,
                )
                move.start()
                moves.append(move)

    def widen(first, count):
        def body(n, carry):
            pair = first + n
            for b in range(z.nq):
                lanes = slice(b * LANES, (b + 1) * LANES)
                edges = hbuf[pl.ds(pl.multiple_of(pair * 8, 8), 8), lanes]
                for k in range(2):
                    t = pair * 2 + k
                    padded[t, b, 8 : 8 + z.cols, :] = vbuf[t, :, lanes].astype(F32)
                    padded[t, b, 6:8, :] = edges[4 * k : 4 * k + 2]
                    padded[t, b, 8 + z.cols : 10 + z.cols, :] = edges[4 * k + 2 : 4 * k + 4]
            return carry

        with jax.named_scope("widen"):
            lax.fori_loop(0, count, body, 0)

    slots = neighbour.shape[1]

    def tile(pairs):
        for m, first in enumerate(pairs):

            def conv_row(k, carry):
                t = first + k
                for b in range(z.nq):
                    lanes = slice(b * LANES, (b + 1) * LANES)
                    total = padded[t + HALO, b, 8 : 8 + z.cols, :]
                    for s in range(slots):
                        at = neighbour[t, s]
                        coef = wrow[basis[t, s], :, lanes] * disco[t, s]
                        total = total + coef * padded[
                            t + at // 5, b, pl.ds(6 + at % 5, z.cols), :
                        ]
                    spatial_out[t, :, lanes] = total.astype(BF16)
                return carry

            with jax.named_scope("conv"):
                lax.fori_loop(0, 2, conv_row, 0)
        with jax.named_scope("mlp"):
            size = 4 * z.cols
            tokens = jnp.concatenate([spatial_out[pl.ds(first, 2)] for first in pairs], axis=0)
            tokens = tokens.reshape(size, z.chan).astype(F32)
            center = jnp.mean(tokens, axis=1, keepdims=True)
            tokens = tokens - center
            spread_ = jnp.mean(tokens * tokens, axis=1, keepdims=True)
            normed = (tokens * lax.rsqrt(spread_ + 1e-05) * gain[...]).astype(BF16)
            hidden = jnp.dot(normed, w_in[...], preferred_element_type=F32) + b_in[...]
            hidden = jax.nn.gelu(hidden).astype(BF16)
            total = jnp.dot(hidden, w_out[...], preferred_element_type=F32) + b_out[...]
            total = total.reshape(4, z.cols, z.chan)
            for m, first in enumerate(pairs):
                skip = fbuf[pl.ds(first, 2)].astype(F32)
                block_out[pl.ds(first, 2)] = (total[2 * m : 2 * m + 2] + skip).astype(BF16)

    with jax.named_scope("h_wait"):
        await_rows(1)
        for move in moves:
            move.wait()
    near = span // 4 - 1
    widen(0, near)
    widen(span // 2 - near, near)

    @pl.when(i == 0)
    def _():
        padded[:HALO] = jnp.zeros((HALO,) + padded.shape[1:], F32)

    @pl.when(i == z.ni - 1)
    def _():
        padded[span - HALO :] = jnp.zeros((HALO,) + padded.shape[1:], F32)

    tile((0, z.rows - 2))
    with jax.named_scope("d_wait"):
        for c in range(2, z.chunks):
            await_rows(c)
    widen(near, span // 2 - 2 * near)

    def rest_tile(n, carry):
        tile((4 * n - 2, 4 * n))
        return carry

    lax.fori_loop(1, z.rows // 4, rest_tile, 0)

    with jax.named_scope("drain"):
        await_bytes(wbuf.at[:, others, :], a_send)
        await_bytes(send1.at[:, pl.ds(0, G - 1)], b_send.at[0])
        await_bytes(send1_late.at[pl.ds(0, G - 1)], b_send.at[1])
        await_bytes(send2.at[:, pl.ds(0, G - 1)], c_send)
        await_bytes(wbuf.at[:, others, :], d_send)
        await_bytes(ebuf.at[:, pl.ds(0, z.nj - 1)], e_send)


def block(z, quad, neighbour, basis, disco, *arrays):
    field, legendre, fr, fi, fwd, inv, weight, gain, w_in, b_in, w_out, b_out = arrays
    hbm = pl.BlockSpec(memory_space=pl.ANY)
    dma = pltpu.SemaphoreType.DMA
    span = z.rows + 2 * HALO

    def vmem(dtype, *dims):
        return pltpu.VMEM(dims, dtype)

    wide = z.groups * z.trow
    return pl.pallas_call(
        functools.partial(block_kernel, z),
        name="block",
        out_shape=(pltpu.VMEM(field.shape, BF16),) * 2,
        in_specs=[hbm] * 4 + [hbm] * len(arrays),
        out_specs=(pl.BlockSpec(memory_space=pltpu.VMEM),) * 2,
        scratch_shapes=[pltpu.SMEM(x.shape, x.dtype) for x in (quad, neighbour, basis, disco)]
        + [
            vmem(BF16, *field.shape),
            vmem(BF16, z.trow, z.nlon, LANES),
            vmem(BF16, z.wper, z.deg, z.nlat),
            vmem(BF16, z.wper, z.nlat, z.deg),
            vmem(BF16, *fwd.shape),
            vmem(BF16, *inv.shape),
            vmem(F32, z.deg, LANES),
            vmem(F32, z.deg, LANES),
            vmem(F32, *weight.shape),
            vmem(F32, *gain.shape),
            vmem(BF16, *w_in.shape),
            vmem(F32, *b_in.shape),
            vmem(BF16, *w_out.shape),
            vmem(F32, *b_out.shape),
            vmem(F32, weight.shape[0], 1, z.chan),
            vmem(F32, z.groups * z.blk, LANES),
            vmem(F32, wide * z.late, LANES),
            vmem(F32, wide * z.early, LANES),
            vmem(F32, wide * z.late, LANES),
            vmem(BF16, z.chunks, z.groups, z.step * z.early, LANES),
            vmem(BF16, z.chunks, z.groups, z.step * z.early, LANES),
            vmem(BF16, z.groups, z.trow * z.late, LANES),
            vmem(BF16, z.groups, z.trow * z.late, LANES),
            vmem(BF16, z.chunks, z.groups, z.blk, LANES),
            vmem(BF16, z.chunks, z.groups, z.blk, LANES),
            vmem(BF16, z.trow, z.nlon, LANES),
            vmem(F32, z.nj * 4 * z.step, LANES),
            vmem(F32, z.chunks, z.nj, 4 * z.step, LANES),
            vmem(BF16, span, z.cols, z.chan),
            vmem(F32, span * 4, z.chan),
            vmem(F32, span, z.nq, z.cols + 16, LANES),
            dma((16,)),
            dma,
            dma((z.chunks,)),
            dma((2,)),
            dma((z.chunks + 1,)),
            dma,
            dma((z.chunks,)),
            dma,
            dma((z.chunks,)),
            dma,
            dma((z.chunks,)),
            dma((2, 2)),
            dma((2, 2)),
        ],
        compiler_params=pltpu.CompilerParams(
            collective_id=0, has_side_effects=True, vmem_limit_bytes=56 << 20
        ),
    )(quad, neighbour, basis, disco, *arrays)


def shards(
    mesh,
    field,
    quad_weight,
    legendre,
    filter_real,
    filter_imag,
    neighbour,
    basis,
    disco_quad,
    disco_weight,
    norm_gain,
    w_in,
    b_in,
    w_out,
    b_out,
):
    lat_rows, lon_cols, channels = field.shape
    z = Sizes(mesh, lat_rows, lon_cols, channels, legendre.shape[0], legendre.shape[1])
    fwd, inv = tables(z.nlon, z.wper * z.groups, z.groups, z.nj)
    return block(
        z,
        quad_weight,
        neighbour,
        basis,
        disco_quad,
        field,
        legendre,
        filter_real,
        filter_imag,
        jnp.asarray(fwd),
        jnp.asarray(inv),
        disco_weight,
        norm_gain[None],
        w_in,
        b_in[None],
        w_out,
        b_out[None],
    )


def solution(mesh):
    placed = (
        P("lat", "lon", None),
        P("lat"),
        P("lat", None, None),
        P(),
        P(),
        P("lat", None),
        P("lat", None),
        P("lat", None),
        P(),
        P(),
        P(),
        P(),
        P(),
        P(),
    )
    return jax.shard_map(
        functools.partial(shards, mesh),
        mesh=mesh,
        in_specs=placed,
        out_specs=(P("lat", "lon", None), P("lat", "lon", None)),
        check_vma=False,
    )
```

time: 107 us -> 97.6 us (0.912)
  the two profiles are of different devices: /device:TPU:1 before, /device:TPU:28 now
where the time goes in v3:
time: 97.6 us
  Pallas kernels  94.9 us (97%)
  local copies, waits for them, and re-layouts  2.03 us (2%)
    pallas_call x1, Pallas kernels, block(): pl.pallas_call(functools.partial(block_kernel, z), name='block', out_shap...  94.9 us
    unnamed x2, local copies, waits for them, and re-layouts  2.03 us

profile of v3, /device:TPU:28, one launch (start us, length us, event | category | flops | bytes accessed | tf_op | source)
XLA Modules:
  0.0 97.6 jit_solution(13503069851857259718)
XLA Ops:
  0.6 94.9 %block.1 = (bf16[12,96,512]{2,1,0:T(8,128)(2,1)S(1)}, bf16[12,96,512]{2,1,0:T(8,128)(2,1)S(1)}) custom-call(f32[12]{0:T(128)} %quad_hbm.1, s32[12,12]{1,0:T(8,128)} %neighbour_hbm.1, s32[12,12]{1,0:T(8,128)} %basis_hbm.1, f32[12,12]{1,0:T(8,128)} %disco_hbm.1, bf16[12,96,512]{2,1,0:T(8,128)(2,1)} %field_ref.1, bf16[12,384,384]{2,1,0:T(8,128)(2,1)} %leg_ref.1, ...), custom_call_target="tpu_custom_call" | custom-call | tf_op jit(solution)/shard_map/block/pallas_call | solution.py:595
  95.5 1.0 %copy.20 = bf16[12,96,512]{2,1,0:T(8,128)(2,1)} copy(bf16[12,96,512]{2,1,0:T(8,128)(2,1)S(1)} %get-tuple-element.2) | data formatting | bytes 2359296
  96.5 1.0 %copy.21 = bf16[12,96,512]{2,1,0:T(8,128)(2,1)} copy(bf16[12,96,512]{2,1,0:T(8,128)(2,1)S(1)} %get-tuple-element.3) | data formatting | bytes 2359296

commit v4 on v3

--- a/solution.py
+++ b/solution.py
@@ -17,7 +17,7 @@
 F32 = jnp.float32
 
 
-def tables(nlon, mmax, groups, blocks):
+def fourier_table(nlon, mmax, groups, blocks):
     per = mmax // groups
     waves = np.stack([np.arange(groups) * per + p for p in range(per)])
     waves = np.repeat(waves[:, None, :], 2, axis=1).reshape(-1)
@@ -26,12 +26,9 @@
     edge = np.array([-2, -1, cols, cols + 1])
     halo = (edge[:, None] + np.arange(blocks)[None, :] * cols).reshape(-1) % nlon
     points = np.concatenate([np.arange(nlon), halo])
-    angle = (waves[:, None] * points[None, :] % nlon) * (2.0 * math.pi / nlon)
-    wave = np.where(part[:, None] == 0, np.cos(angle), -np.sin(angle)) / math.sqrt(nlon)
-    factor = np.where(waves == 0, 1.0, 2.0)
-    forward = wave[:, :nlon].astype(ml_dtypes.bfloat16)
-    inverse = (wave * factor[:, None]).T.astype(ml_dtypes.bfloat16)
-    return forward, np.ascontiguousarray(inverse)
+    angle = (points[:, None] * waves[None, :] % nlon) * (2.0 * math.pi / nlon)
+    wave = np.where(part[None, :] == 0, np.cos(angle), -np.sin(angle)) / math.sqrt(nlon)
+    return wave.astype(ml_dtypes.bfloat16)
 
 
 class Sizes:
@@ -71,7 +68,6 @@
     leg_ref,
     fr_ref,
     fi_ref,
-    fwd_ref,
     inv_ref,
     weight_ref,
     gain_ref,
@@ -86,6 +82,7 @@
     basis,
     disco,
     fbuf,
+    fblocks,
     cols_in,
     ltab,
     ltrans,
@@ -147,7 +144,7 @@
 
     field_load = load(0, field_ref, fbuf)
     leg_load = load(1, leg_ref.at[pl.ds(h * z.wper, z.wper)], ltab)
-    fwd_load = load(2, fwd_ref, fwd)
+    table_load = load(2, inv_ref, inv)
 
     low = G // z.deep // 2
     deep = lax.rem(lax.div(me, low), z.deep)
@@ -197,7 +194,6 @@
         load(n + 3, src, dst)
         for n, (src, dst) in enumerate(
             (
-                (inv_ref, inv),
                 (fr_ref.at[:, pl.ds(lane0, LANES)], gr),
                 (fi_ref.at[:, pl.ds(lane0, LANES)], gi),
                 (weight_ref, weight),
@@ -214,7 +210,12 @@
         )
     ]
     field_load.wait()
-    cols_in[:, here, :] = fbuf[pl.ds(h * z.trow, z.trow), :, pl.ds(lane0, LANES)]
+    for b in range(z.nq):
+        fblocks[b] = fbuf[:, :, b * LANES : (b + 1) * LANES]
+    cols_in[:, here, :] = fblocks[q, pl.ds(h * z.trow, z.trow)]
+    table_load.wait()
+    with jax.named_scope("trans"):
+        fwd[...] = inv[: z.nlon, :].T
     with jax.named_scope("barrier"):
         pl.semaphore_wait(barrier, lon_only + G - 1)
 
@@ -224,11 +225,7 @@
             hp = lax.div(p, z.nq)
             qp = lax.rem(p, z.nq)
             pltpu.make_async_remote_copy(
-                src_ref=fbuf.at[
-                    pl.ds(hp * z.trow + c * step, step),
-                    :,
-                    pl.ds(pl.multiple_of(qp * LANES, LANES), LANES),
-                ],
+                src_ref=fblocks.at[qp, pl.ds(hp * z.trow + c * step, step)],
                 dst_ref=cols_in.at[pl.ds(c * step, step), here, :],
                 send_sem=a_send,
                 recv_sem=a_recv.at[c],
@@ -250,11 +247,10 @@
     with jax.named_scope("trans"):
         for w in range(z.wper):
             ltrans[w] = ltab[w].T
-    rest[3].wait()
-    rest[9].wait()
+    rest[2].wait()
+    rest[8].wait()
     for r in range(weight.shape[0]):
         wrow[r] = weight[r : r + 1, :]
-    fwd_load.wait()
 
     def each_group(act):
         def body(s, carry):
@@ -316,7 +312,7 @@
         b_recv.at[z.chunks],
     )
 
-    for copy in rest[1:3]:
+    for copy in rest[:2]:
         copy.wait()
 
     def legendre(buf, count, first):
@@ -331,10 +327,11 @@
             b = gi[...]
             filt = jnp.concatenate([a * re - b * im, a * im + b * re], axis=1).astype(BF16)
             syn = jnp.dot(ltrans[first + w], filt, preferred_element_type=F32)
+            twice = jnp.where(me + first + w == 0, 1.0, 2.0) if first + w == 0 else 2.0
             for r in range(2):
-                buf[pl.ds(2 * w + r, z.nlat, stride=count), :] = syn[
-                    :, r * LANES : (r + 1) * LANES
-                ]
+                buf[pl.ds(2 * w + r, z.nlat, stride=count), :] = (
+                    syn[:, r * LANES : (r + 1) * LANES] * twice
+                )
 
     def pack_back(buf, count, c, at):
         def pack(s):
@@ -392,7 +389,7 @@
     edge_rows = 4 * step
     span = z.rows + 2 * HALO
     moves = []
-    for copy in rest[:1] + rest[4:9] + rest[10:]:
+    for copy in rest[3:8] + rest[9:]:
         copy.wait()
 
     def await_rows(c):
@@ -442,7 +439,7 @@
             for src, dst, ss, rs in (
                 (
                     wbuf.at[pl.ds(c * step, step), there, :],
-                    vbuf.at[pl.ds(row, step), :, lanes],
+                    vbuf.at[q, pl.ds(row, step)],
                     d_send,
                     d_recv.at[c],
                 ),
@@ -461,7 +458,7 @@
         lax.fori_loop(1, z.nj, send_d, 0)
         if c + 2 < z.chunks:
             spread_back(c + 2)
-        vbuf[pl.ds(row, step), :, lanes] = wbuf[pl.ds(c * step, step), here, :]
+        vbuf[q, pl.ds(row, step)] = wbuf[pl.ds(c * step, step), here, :]
         hbuf[edge_at, lanes] = ebuf[c, j]
 
         if c != 1:
@@ -474,7 +471,7 @@
         ):
             for f, (src, dst) in enumerate(
                 (
-                    (vbuf.at[pl.ds(src_row, HALO)], vbuf.at[pl.ds(dst_row, HALO)]),
+                    (vbuf.at[:, pl.ds(src_row, HALO)], vbuf.at[:, pl.ds(dst_row, HALO)]),
                     (
                         hbuf.at[pl.ds(src_row * 4, HALO * 4)],
                         hbuf.at[pl.ds(dst_row * 4, HALO * 4)],
@@ -500,7 +497,7 @@
                 edges = hbuf[pl.ds(pl.multiple_of(pair * 8, 8), 8), lanes]
                 for k in range(2):
                     t = pair * 2 + k
-                    padded[t, b, 8 : 8 + z.cols, :] = vbuf[t, :, lanes].astype(F32)
+                    padded[t, b, 8 : 8 + z.cols, :] = vbuf[b, t].astype(F32)
                     padded[t, b, 6:8, :] = edges[4 * k : 4 * k + 2]
                     padded[t, b, 8 + z.cols : 10 + z.cols, :] = edges[4 * k + 2 : 4 * k + 4]
             return carry
@@ -511,24 +508,24 @@
     slots = neighbour.shape[1]
 
     def tile(pairs):
-        for m, first in enumerate(pairs):
-
-            def conv_row(k, carry):
-                t = first + k
-                for b in range(z.nq):
-                    lanes = slice(b * LANES, (b + 1) * LANES)
-                    total = padded[t + HALO, b, 8 : 8 + z.cols, :]
-                    for s in range(slots):
-                        at = neighbour[t, s]
-                        coef = wrow[basis[t, s], :, lanes] * disco[t, s]
-                        total = total + coef * padded[
-                            t + at // 5, b, pl.ds(6 + at % 5, z.cols), :
-                        ]
-                    spatial_out[t, :, lanes] = total.astype(BF16)
-                return carry
-
-            with jax.named_scope("conv"):
-                lax.fori_loop(0, 2, conv_row, 0)
+        def conv_row(t):
+            taps = []
+            for s in range(slots):
+                at = neighbour[t, s]
+                down = lax.div(at, 5)
+                taps.append((t + down, 6 + at - 5 * down, basis[t, s], disco[t, s]))
+            for b in range(z.nq):
+                lanes = slice(b * LANES, (b + 1) * LANES)
+                total = padded[t + HALO, b, 8 : 8 + z.cols, :]
+                for row, col, kind, amount in taps:
+                    coef = wrow[kind, :, lanes] * amount
+                    total = total + coef * padded[row, b, pl.ds(col, z.cols), :]
+                spatial_out[t, :, lanes] = total.astype(BF16)
+
+        with jax.named_scope("conv"):
+            for first in pairs:
+                for k in range(2):
+                    conv_row(first + k)
         with jax.named_scope("mlp"):
             size = 4 * z.cols
             tokens = jnp.concatenate([spatial_out[pl.ds(first, 2)] for first in pairs], axis=0)
@@ -583,7 +580,7 @@
 
 
 def block(z, quad, neighbour, basis, disco, *arrays):
-    field, legendre, fr, fi, fwd, inv, weight, gain, w_in, b_in, w_out, b_out = arrays
+    field, legendre, fr, fi, inv, weight, gain, w_in, b_in, w_out, b_out = arrays
     hbm = pl.BlockSpec(memory_space=pl.ANY)
     dma = pltpu.SemaphoreType.DMA
     span = z.rows + 2 * HALO
@@ -601,10 +598,11 @@
         scratch_shapes=[pltpu.SMEM(x.shape, x.dtype) for x in (quad, neighbour, basis, disco)]
         + [
             vmem(BF16, *field.shape),
+            vmem(BF16, z.nq, z.rows, z.cols, LANES),
             vmem(BF16, z.trow, z.nlon, LANES),
             vmem(BF16, z.wper, z.deg, z.nlat),
             vmem(BF16, z.wper, z.nlat, z.deg),
-            vmem(BF16, *fwd.shape),
+            vmem(BF16, inv.shape[1], z.nlon),
             vmem(BF16, *inv.shape),
             vmem(F32, z.deg, LANES),
             vmem(F32, z.deg, LANES),
@@ -628,7 +626,7 @@
             vmem(BF16, z.trow, z.nlon, LANES),
             vmem(F32, z.nj * 4 * z.step, LANES),
             vmem(F32, z.chunks, z.nj, 4 * z.step, LANES),
-            vmem(BF16, span, z.cols, z.chan),
+            vmem(BF16, z.nq, span, z.cols, LANES),
             vmem(F32, span * 4, z.chan),
             vmem(F32, span, z.nq, z.cols + 16, LANES),
             dma((16,)),
@@ -670,7 +668,7 @@
 ):
     lat_rows, lon_cols, channels = field.shape
     z = Sizes(mesh, lat_rows, lon_cols, channels, legendre.shape[0], legendre.shape[1])
-    fwd, inv = tables(z.nlon, z.wper * z.groups, z.groups, z.nj)
+    table = fourier_table(z.nlon, z.wper * z.groups, z.groups, z.nj)
     return block(
         z,
         quad_weight,
@@ -681,8 +679,7 @@
         legendre,
         filter_real,
         filter_imag,
-        jnp.asarray(fwd),
-        jnp.asarray(inv),
+        jnp.asarray(table),
         disco_weight,
         norm_gain[None],
         w_in,

time: 97.6 us -> 95.6 us (0.980)
  the two profiles are of different devices: /device:TPU:28 before, /device:TPU:1 now
where the time goes in v4:
time: 95.6 us; the launch traced here: 93.9 us
  Pallas kernels  91.2 us (95%)
  local copies, waits for them, and re-layouts  2.03 us (2%)
    pallas_call x1, Pallas kernels, block(): pl.pallas_call(functools.partial(block_kernel, z), name='block', out_shap...  91.2 us
    unnamed x2, local copies, waits for them, and re-layouts  2.03 us

profile of v4, /device:TPU:1, one launch (start us, length us, event | category | flops | bytes accessed | tf_op | source)
XLA Modules:
  0.0 93.9 jit_solution(16893447264401609582)
XLA Ops:
  0.6 91.2 %block.1 = (bf16[12,96,512]{2,1,0:T(8,128)(2,1)S(1)}, bf16[12,96,512]{2,1,0:T(8,128)(2,1)S(1)}) custom-call(f32[12]{0:T(128)} %quad_hbm.1, s32[12,12]{1,0:T(8,128)} %neighbour_hbm.1, s32[12,12]{1,0:T(8,128)} %basis_hbm.1, f32[12,12]{1,0:T(8,128)} %disco_hbm.1, bf16[12,96,512]{2,1,0:T(8,128)(2,1)} %field_ref.1, bf16[12,384,384]{2,1,0:T(8,128)(2,1)} %leg_ref.1, ...), custom_call_target="tpu_custom_call" | custom-call | tf_op jit(solution)/shard_map/block/pallas_call | solution.py:592
  91.9 1.0 %copy.19 = bf16[12,96,512]{2,1,0:T(8,128)(2,1)} copy(bf16[12,96,512]{2,1,0:T(8,128)(2,1)S(1)} %get-tuple-element.2) | data formatting | bytes 2359296
  92.9 1.0 %copy.20 = bf16[12,96,512]{2,1,0:T(8,128)(2,1)} copy(bf16[12,96,512]{2,1,0:T(8,128)(2,1)S(1)} %get-tuple-element.3) | data formatting | bytes 2359296
